TPU v7x, 256 devices: a whole 4x4x8 slice. The times are simulated.
256 devices in a mesh: rows: 8 (over x_hi, y), cols: 32 (over z, x_lo, core).
Axes of the slice: x: 4 (x_hi: 2, x_lo: 2; x = x_hi * 2 + x_lo), y: 4, z: 8, core: 2. Of those that a mesh axis runs over, the one named last changes fastest.
Arguments:
- features: bfloat16 [4, 256, 64, 4096], P(None, None, 'rows', 'cols'), may hold values from -8 to 8
- cotangent: bfloat16 [4, 256, 64, 4096], P(None, None, 'rows', 'cols'), may hold values from -6 to 6
- reduce_weight: bfloat16 [256, 64], replicated, may hold values from -0.375 to 0.375
- spatial_weight: bfloat16 [9, 64, 64], replicated, may hold values from -0.25 to 0.25
- expand_weight: bfloat16 [64, 256], replicated, may hold values from -0.75 to 0.75
- reduce_factor: float32 [4, 256], replicated, may hold values from 0.25 to 1.75
- spatial_factor: float32 [4, 64], replicated, may hold values from 0.25 to 1.75
- expand_factor: float32 [4, 64], replicated, may hold values from 0.25 to 1.75
- output_factor: float32 [4, 256], replicated, may hold values from 0.25 to 1.75
- gain_first: float32 [64], replicated, may hold values from 0.25 to 1.75
- shift_first: float32 [64], replicated, may hold values from -3 to 3
- gain_second: float32 [64], replicated, may hold values from 0.25 to 1.75
- shift_second: float32 [64], replicated, may hold values from -3 to 3
Outputs:
- grad_features: bfloat16 [4, 256, 64, 4096], P(None, None, 'rows', 'cols')
- grad_reduce: float32 [256, 64], replicated
- grad_spatial: float32 [9, 64, 64], replicated
- grad_expand: float32 [64, 256], replicated
- grad_reduce_factor: float32 [4, 256], replicated
- grad_spatial_factor: float32 [4, 64], replicated
- grad_expand_factor: float32 [4, 64], replicated
- grad_output_factor: float32 [4, 256], replicated
- grad_gain_first: float32 [64], replicated
- grad_shift_first: float32 [64], replicated
- grad_gain_second: float32 [64], replicated
- grad_shift_second: float32 [64], replicated
All inputs are finite; a program needn't handle non-finite values.
Results may differ from a plain program's by a relative error of at most 0.01.
Values may be sent and summed in bfloat16 or wider, within the bound.
A program may use at most 128 MiB of HBM per device.

v0:
```python
import functools

import jax
import jax.numpy as jnp
from jax import lax
from jax.sharding import Mesh
from jax.sharding import PartitionSpec as P

ROWS_COLS = ("rows_0", "rows_1", "cols_0", "cols_1", "cols_2")
ROWS = ("rows_0", "rows_1")
COLS = ("cols_0", "cols_1", "cols_2")


EPSILON = 1e-05


def by_axis(array, axes):
    return functools.reduce(lax.psum, axes, array)


def with_halo(cells, sides, width):
    for axis, dim in sides:
        count = lax.axis_size(axis)
        ends = count - 1
        head = lax.slice_in_dim(cells, 0, width, axis=dim)
        tail = lax.slice_in_dim(cells, cells.shape[dim] - width, cells.shape[dim], axis=dim)
        cells = jnp.concatenate(
            [
                lax.ppermute(tail, axis, [(i, (i + 1) % count) for i in range(ends)]),
                cells,
                lax.ppermute(head, axis, [((i + 1) % count, i) for i in range(ends)]),
            ],
            axis=dim,
        )
    return cells


def packed_total(arrays, axis):
    flat, at, finished = (jnp.concatenate([a.reshape(-1) for a in arrays]), 0, [])
    so_far = lax.psum(flat, axis)
    for a in arrays:
        finished.append(so_far[at : at + a.size].reshape(a.shape))
        at += a.size
    return tuple(finished)


def activate(value):
    return value * jax.nn.sigmoid(value)


def slope(value):
    sig = jax.nn.sigmoid(value)
    return sig * (1.0 + value * (1.0 - sig))


def norm_forward(acts, gain, shift, count):
    total, square = (
        by_axis(jnp.sum(acts, axis=2), ROWS_COLS),
        by_axis(jnp.sum(acts * acts, axis=2), ROWS_COLS),
    )
    mean = total / count
    var = square / count - mean * mean
    centred = acts - mean[:, :, None]
    rstd = lax.rsqrt(var + EPSILON)[:, :, None]
    normed = centred * rstd
    pre = gain[None, :, None] * normed + shift[None, :, None]
    return (activate(pre).astype(jnp.bfloat16), normed, pre, rstd)


def norm_backward(upstream, normed, pre, rstd, gain, count):
    dpre = upstream * slope(pre)
    plain, weighted = (
        by_axis(jnp.sum(dpre, axis=2), ROWS_COLS),
        by_axis(jnp.sum(dpre * normed, axis=2), ROWS_COLS),
    )
    dact = (
        gain[None, :, None]
        * rstd
        * (dpre - plain[:, :, None] / count - normed * weighted[:, :, None] / count)
    )
    return (dact, jnp.sum(weighted, axis=0), jnp.sum(plain, axis=0))


def rim_cells(field):
    return with_halo(field, ((ROWS, 2), (COLS, 3)), 1)


def rim_grads(field):
    return with_halo(field, ((ROWS, 2), (COLS, 3)), 1)


def conv_forward(padded, weights, tall, broad):
    members, narrow = (padded.shape[0], padded.shape[1])
    total = None
    for tap in range(9):
        row_off, col_off = (tap // 3, tap % 3)
        window = padded[:, :, row_off : row_off + tall, col_off : col_off + broad].reshape(
            members, narrow, tall * broad
        )
        term = jnp.einsum(
            "mfo,mfp->mop", weights[:, tap], window, preferred_element_type=jnp.float32
        )
        total = term if total is None else total + term
    return total


def conv_backward(padded_back, padded_one, weights, dact_low, tall, broad):
    members, narrow = (padded_back.shape[0], padded_back.shape[1])
    total = None
    pieces = []
    for tap in range(9):
        row_off, col_off = (tap // 3, tap % 3)
        flipped = padded_back[
            :, :, 2 - row_off : 2 - row_off + tall, 2 - col_off : 2 - col_off + broad
        ].reshape(members, narrow, tall * broad)
        term = jnp.einsum(
            "mfo,mop->mfp", weights[:, tap], flipped, preferred_element_type=jnp.float32
        )
        total = term if total is None else total + term
        window = padded_one[:, :, row_off : row_off + tall, col_off : col_off + broad].reshape(
            members, narrow, tall * broad
        )
        pieces.append(
            jnp.einsum("mfp,mop->mfo", window, dact_low, preferred_element_type=jnp.float32)
        )
    return (total, jnp.stack(pieces, axis=1))


def fold_members(
    part_reduce,
    part_spatial,
    part_expand,
    rw,
    sw,
    ew,
    reduce_factor,
    spatial_factor,
    expand_factor,
    output_factor,
):
    grad_reduce = jnp.sum(part_reduce * reduce_factor[:, :, None], axis=0)
    grad_reduce_factor = jnp.sum(part_reduce * rw[None], axis=2)
    grad_spatial = jnp.sum(part_spatial * spatial_factor[:, None, :, None], axis=0)
    grad_spatial_factor = jnp.sum(part_spatial * sw[None], axis=(1, 3))
    grad_expand = jnp.sum(
        part_expand * expand_factor[:, :, None] * output_factor[:, None, :], axis=0
    )
    grad_expand_factor = jnp.sum(part_expand * ew[None] * output_factor[:, None, :], axis=2)
    grad_output_factor = jnp.sum(part_expand * ew[None] * expand_factor[:, :, None], axis=1)
    return (
        grad_reduce,
        grad_spatial,
        grad_expand,
        grad_reduce_factor,
        grad_spatial_factor,
        grad_expand_factor,
        grad_output_factor,
    )


def body(
    features,
    cotangent,
    reduce_weight,
    spatial_weight,
    expand_weight,
    reduce_factor,
    spatial_factor,
    expand_factor,
    output_factor,
    gain_first,
    shift_first,
    gain_second,
    shift_second,
):
    members, channels, tall, broad = features.shape
    narrow = reduce_weight.shape[1]
    cells = tall * broad
    count = float(cells * lax.axis_size(ROWS) * lax.axis_size(COLS))
    rw = reduce_weight.astype(jnp.float32)
    sw = spatial_weight.astype(jnp.float32)
    ew = expand_weight.astype(jnp.float32)
    member_reduce = (reduce_factor[:, :, None] * rw[None]).astype(jnp.bfloat16)
    member_spatial = (spatial_factor[:, None, :, None] * sw[None]).astype(jnp.bfloat16)
    member_expand = (expand_factor[:, :, None] * ew[None] * output_factor[:, None, :]).astype(
        jnp.bfloat16
    )
    flat = features.reshape(members, channels, cells)
    first = jnp.einsum("mcf,mcp->mfp", member_reduce, flat, preferred_element_type=jnp.float32)
    hidden_one, normed_one, pre_one, rstd_one = norm_forward(first, gain_first, shift_first, count)
    padded_one = rim_cells(hidden_one.reshape(members, narrow, tall, broad))
    second = conv_forward(padded_one, member_spatial, tall, broad)
    hidden_two, normed_two, pre_two, rstd_two = norm_forward(
        second, gain_second, shift_second, count
    )
    third = jnp.einsum(
        "mfc,mfp->mcp", member_expand, hidden_two, preferred_element_type=jnp.float32
    )
    summed = flat.astype(jnp.float32) + third
    upstream = cotangent.reshape(members, channels, cells).astype(jnp.float32) * slope(summed)
    upstream_low = upstream.astype(jnp.bfloat16)
    back_two = jnp.einsum(
        "mfc,mcp->mfp", member_expand, upstream_low, preferred_element_type=jnp.float32
    )
    part_expand = jnp.einsum(
        "mfp,mcp->mfc", hidden_two, upstream_low, preferred_element_type=jnp.float32
    )
    dact_two, grad_gain_second, grad_shift_second = norm_backward(
        back_two, normed_two, pre_two, rstd_two, gain_second, count
    )
    dact_two_low = dact_two.astype(jnp.bfloat16)
    padded_back = rim_grads(dact_two_low.reshape(members, narrow, tall, broad))
    back_one, part_spatial = conv_backward(
        padded_back, padded_one, member_spatial, dact_two_low, tall, broad
    )
    dact_one, grad_gain_first, grad_shift_first = norm_backward(
        back_one, normed_one, pre_one, rstd_one, gain_first, count
    )
    dact_one_low = dact_one.astype(jnp.bfloat16)
    grad_flat = upstream + jnp.einsum(
        "mcf,mfp->mcp", member_reduce, dact_one_low, preferred_element_type=jnp.float32
    )
    grad_features = grad_flat.astype(jnp.bfloat16).reshape(members, channels, tall, broad)
    part_reduce = jnp.einsum("mcp,mfp->mcf", flat, dact_one_low, preferred_element_type=jnp.float32)
    local = fold_members(
        part_reduce,
        part_spatial,
        part_expand,
        rw,
        sw,
        ew,
        reduce_factor,
        spatial_factor,
        expand_factor,
        output_factor,
    )
    totals = packed_total(
        (local[0], local[1], local[2], local[3], local[4], local[5], local[6]), ROWS_COLS
    )
    return (
        grad_features,
        totals[0],
        totals[1],
        totals[2],
        totals[3],
        totals[4],
        totals[5],
        totals[6],
        grad_gain_first,
        grad_shift_first,
        grad_gain_second,
        grad_shift_second,
    )


def solution(mesh):
    split = Mesh(
        mesh.devices.reshape(2, 4, 8, 2, 2), ("rows_0", "rows_1", "cols_0", "cols_1", "cols_2")
    )
    placed = (
        P(None, None, ROWS, COLS),
        P(None, None, ROWS, COLS),
        P(),
        P(),
        P(),
        P(),
        P(),
        P(),
        P(),
        P(),
        P(),
        P(),
        P(),
    )
    return jax.shard_map(
        body,
        mesh=split,
        in_specs=placed,
        out_specs=(
            P(None, None, ROWS, COLS),
            P(),
            P(),
            P(),
            P(),
            P(),
            P(),
            P(),
            P(),
            P(),
            P(),
            P(),
        ),
        check_vma=False,
    )
```

profile of v0, /device:TPU:1, one launch (start us, length us, event | category | flops | bytes accessed | tf_op | source)
XLA Modules:
  0.0 572.1 jit_solution(7597058974139156140)
XLA Ops:
  7.2 2.8 reshape.206
  10.8 5.9 %all-reduce.19 = (f32[4,64]{1,0:T(4,128)S(1)}, f32[4,64]{1,0:T(4,128)S(1)}) all-reduce(f32[4,64]{1,0:T(4,128)S(1)} %get-tuple-element.57, f32[4,64]{1,0:T(4,128)S(1)} %get-tuple-element.56), channel_id=1, replica_groups=mesh['rows_0'=2,'rows_1'=4,'cols_0'=8,'cols_1'=2,'cols_2'=2] {'rows_0'}, use_global_device_ids=true, to_apply=%region_7.0 | all-reduce | flops 512 | bytes 4096 | tf_op jit(solution)/shard_map/psum | solution.py:18
  16.6 8.9 %all-reduce.7 = (f32[4,64]{1,0:T(4,128)S(1)}, f32[4,64]{1,0:T(4,128)S(1)}) all-reduce(f32[4,64]{1,0:T(4,128)S(1)} %get-tuple-element.101, f32[4,64]{1,0:T(4,128)S(1)} %get-tuple-element.102), channel_id=1, replica_groups=mesh['rows_0'=2,'rows_1'=4,'cols_0'=8,'cols_1'=2,'cols_2'=2] {'rows_1'}, use_global_device_ids=true, to_apply=%region_8.0 | all-reduce | flops 512 | bytes 4096 | tf_op jit(solution)/shard_map/psum | solution.py:18
  25.6 16.2 %all-reduce.3 = (f32[4,64]{1,0:T(4,128)S(1)}, f32[4,64]{1,0:T(4,128)S(1)}) all-reduce(f32[4,64]{1,0:T(4,128)S(1)} %get-tuple-element.77, f32[4,64]{1,0:T(4,128)S(1)} %get-tuple-element.78), channel_id=1, replica_groups=mesh['rows_0'=2,'rows_1'=4,'cols_0'=8,'cols_1'=2,'cols_2'=2] {'cols_0'}, use_global_device_ids=true, to_apply=%region_9.0 | all-reduce | flops 512 | bytes 4096 | tf_op jit(solution)/shard_map/psum | solution.py:18
  41.8 3.8 all-reduce.15
  45.5 10.9 %all-reduce.11 = (f32[4,64]{1,0:T(4,128)S(1)}, f32[4,64]{1,0:T(4,128)S(1)}) all-reduce(f32[4,64]{1,0:T(4,128)S(1)} %get-tuple-element.93, f32[4,64]{1,0:T(4,128)S(1)} %get-tuple-element.94), channel_id=1, replica_groups=mesh['rows_0'=2,'rows_1'=4,'cols_0'=8,'cols_1'=2,'cols_2'=2] {'cols_2'}, use_global_device_ids=true, to_apply=%region_11.0 | all-reduce | flops 512 | bytes 4096 | tf_op jit(solution)/shard_map/psum | solution.py:18
  58.2 1.9 copy.81
  60.8 1.9 collective-permute-start
  62.8 1.3 collective-permute-start.1
  66.7 4.5 reshape.237
  71.9 3.5 collective-permute-start.2
  75.5 1.9 collective-permute-start.3
  77.4 1.8 copy.85
  79.2 1.8 copy.90
  80.9 2.8 pad_maximum_fusion.4
  83.7 2.1 reshape.209
  85.8 2.1 reshape.214
  87.8 5.0 pad_maximum_fusion
  92.9 4.2 fusion.42
  97.1 1.6 copy.124
  98.7 2.5 copy.125
  101.2 2.3 copy.126
  108.9 2.3 copy.127
  111.2 2.3 copy.128
  113.5 2.3 copy.129
  115.8 1.7 convolution_add_fusion.10
  119.6 1.3 fusion.38
  120.8 10.8 %all-reduce.18 = (f32[4,64]{1,0:T(4,128)S(1)}, f32[4,64]{1,0:T(4,128)S(1)}) all-reduce(f32[4,64]{1,0:T(4,128)S(1)} %get-tuple-element.55, f32[4,64]{1,0:T(4,128)S(1)} %get-tuple-element.54), channel_id=1, replica_groups=mesh['rows_0'=2,'rows_1'=4,'cols_0'=8,'cols_1'=2,'cols_2'=2] {'rows_0'}, use_global_device_ids=true, to_apply=%region_19.0 | all-reduce | flops 512 | bytes 4096 | tf_op jit(solution)/shard_map/psum | solution.py:18
  131.7 7.4 %all-reduce.6 = (f32[4,64]{1,0:T(4,128)S(1)}, f32[4,64]{1,0:T(4,128)S(1)}) all-reduce(f32[4,64]{1,0:T(4,128)S(1)} %get-tuple-element.99, f32[4,64]{1,0:T(4,128)S(1)} %get-tuple-element.100), channel_id=1, replica_groups=mesh['rows_0'=2,'rows_1'=4,'cols_0'=8,'cols_1'=2,'cols_2'=2] {'rows_1'}, use_global_device_ids=true, to_apply=%region_20.0 | all-reduce | flops 512 | bytes 4096 | tf_op jit(solution)/shard_map/psum | solution.py:18
  139.1 10.7 %all-reduce.2 = (f32[4,64]{1,0:T(4,128)S(1)}, f32[4,64]{1,0:T(4,128)S(1)}) all-reduce(f32[4,64]{1,0:T(4,128)S(1)} %get-tuple-element.75, f32[4,64]{1,0:T(4,128)S(1)} %get-tuple-element.76), channel_id=1, replica_groups=mesh['rows_0'=2,'rows_1'=4,'cols_0'=8,'cols_1'=2,'cols_2'=2] {'cols_0'}, use_global_device_ids=true, to_apply=%region_21.0 | all-reduce | flops 512 | bytes 4096 | tf_op jit(solution)/shard_map/psum | solution.py:18
  149.7 3.8 all-reduce.14
  153.5 12.3 %all-reduce.10 = (f32[4,64]{1,0:T(4,128)S(1)}, f32[4,64]{1,0:T(4,128)S(1)}) all-reduce(f32[4,64]{1,0:T(4,128)S(1)} %get-tuple-element.91, f32[4,64]{1,0:T(4,128)S(1)} %get-tuple-element.92), channel_id=1, replica_groups=mesh['rows_0'=2,'rows_1'=4,'cols_0'=8,'cols_1'=2,'cols_2'=2] {'cols_2'}, use_global_device_ids=true, to_apply=%region_23.0 | all-reduce | flops 512 | bytes 4096 | tf_op jit(solution)/shard_map/psum | solution.py:18
  165.9 4.7 multiply_multiply_fusion
  170.6 2.0 multiply_reduce_fusion.6
  172.6 2.0 fusion.37
  174.6 5.8 %all-reduce.17 = (f32[4,64]{1,0:T(4,128)S(1)}, f32[4,64]{1,0:T(4,128)}) all-reduce(f32[4,64]{1,0:T(4,128)S(1)} %get-tuple-element.53, f32[4,64]{1,0:T(4,128)S(1)} %get-tuple-element.52), channel_id=1, replica_groups=mesh['rows_0'=2,'rows_1'=4,'cols_0'=8,'cols_1'=2,'cols_2'=2] {'rows_0'}, use_global_device_ids=true, to_apply=%region_31.0 | all-reduce | flops 512 | bytes 4096 | tf_op jit(solution)/shard_map/psum | solution.py:18
  180.4 6.1 %all-reduce.5 = (f32[4,64]{1,0:T(4,128)S(1)}, f32[4,64]{1,0:T(4,128)S(1)}) all-reduce(f32[4,64]{1,0:T(4,128)S(1)} %get-tuple-element.97, f32[4,64]{1,0:T(4,128)} %get-tuple-element.98), channel_id=1, replica_groups=mesh['rows_0'=2,'rows_1'=4,'cols_0'=8,'cols_1'=2,'cols_2'=2] {'rows_1'}, use_global_device_ids=true, to_apply=%region_32.0 | all-reduce | flops 512 | bytes 4096 | tf_op jit(solution)/shard_map/psum | solution.py:18
  186.5 13.4 %all-reduce.1 = (f32[4,64]{1,0:T(4,128)S(1)}, f32[4,64]{1,0:T(4,128)}) all-reduce(f32[4,64]{1,0:T(4,128)S(1)} %get-tuple-element.73, f32[4,64]{1,0:T(4,128)S(1)} %get-tuple-element.74), channel_id=1, replica_groups=mesh['rows_0'=2,'rows_1'=4,'cols_0'=8,'cols_1'=2,'cols_2'=2] {'cols_0'}, use_global_device_ids=true, to_apply=%region_33.0 | all-reduce | flops 512 | bytes 4096 | tf_op jit(solution)/shard_map/psum | solution.py:18
  199.9 3.9 all-reduce.13
  203.8 10.6 %all-reduce.9 = (f32[4,64]{1,0:T(4,128)S(1)}, f32[4,64]{1,0:T(4,128)}) all-reduce(f32[4,64]{1,0:T(4,128)S(1)} %get-tuple-element.89, f32[4,64]{1,0:T(4,128)S(1)} %get-tuple-element.90), channel_id=1, replica_groups=mesh['rows_0'=2,'rows_1'=4,'cols_0'=8,'cols_1'=2,'cols_2'=2] {'cols_2'}, use_global_device_ids=true, to_apply=%region_35.0 | all-reduce | flops 512 | bytes 4096 | tf_op jit(solution)/shard_map/psum | solution.py:18
  214.4 1.3 fusion.49
  215.7 1.9 multiply_convert_fusion.2
  217.9 1.4 fusion.33
  224.2 1.9 copy.92
  226.9 4.3 collective-permute-start.4
  231.2 1.4 collective-permute-start.5
  232.6 2.3 multiply_reduce_fusion
  238.7 3.4 collective-permute-start.6
  242.1 2.4 collective-permute-start.7
  246.7 2.8 pad_maximum_fusion.2
  249.5 2.1 reshape.218
  251.5 2.1 reshape.223
  253.6 5.2 maximum_maximum_fusion.1
  258.9 1.4 fusion.41
  266.9 1.9 fusion.36
  268.8 7.9 %all-reduce.16 = (f32[4,64]{1,0:T(4,128)S(1)}, f32[4,64]{1,0:T(4,128)S(1)}) all-reduce(f32[4,64]{1,0:T(4,128)S(1)} %get-tuple-element.51, f32[4,64]{1,0:T(4,128)S(1)} %get-tuple-element.50), channel_id=1, replica_groups=mesh['rows_0'=2,'rows_1'=4,'cols_0'=8,'cols_1'=2,'cols_2'=2] {'rows_0'}, use_global_device_ids=true, to_apply=%region_43.0 | all-reduce | flops 512 | bytes 4096 | tf_op jit(solution)/shard_map/psum | solution.py:18
  276.7 9.6 %all-reduce.4 = (f32[4,64]{1,0:T(4,128)S(1)}, f32[4,64]{1,0:T(4,128)S(1)}) all-reduce(f32[4,64]{1,0:T(4,128)S(1)} %get-tuple-element.95, f32[4,64]{1,0:T(4,128)S(1)} %get-tuple-element.96), channel_id=1, replica_groups=mesh['rows_0'=2,'rows_1'=4,'cols_0'=8,'cols_1'=2,'cols_2'=2] {'rows_1'}, use_global_device_ids=true, to_apply=%region_44.0 | all-reduce | flops 512 | bytes 4096 | tf_op jit(solution)/shard_map/psum | solution.py:18
  286.2 10.8 %all-reduce = (f32[4,64]{1,0:T(4,128)S(1)}, f32[4,64]{1,0:T(4,128)S(1)}) all-reduce(f32[4,64]{1,0:T(4,128)S(1)} %get-tuple-element.71, f32[4,64]{1,0:T(4,128)S(1)} %get-tuple-element.72), channel_id=1, replica_groups=mesh['rows_0'=2,'rows_1'=4,'cols_0'=8,'cols_1'=2,'cols_2'=2] {'cols_0'}, use_global_device_ids=true, to_apply=%region_45.0 | all-reduce | flops 512 | bytes 4096 | tf_op jit(solution)/shard_map/psum | solution.py:18
  297.0 5.1 all-reduce.12
  302.1 8.7 %all-reduce.8 = (f32[4,64]{1,0:T(4,128)S(1)}, f32[4,64]{1,0:T(4,128)S(1)}) all-reduce(f32[4,64]{1,0:T(4,128)S(1)} %get-tuple-element.87, f32[4,64]{1,0:T(4,128)S(1)} %get-tuple-element.88), channel_id=1, replica_groups=mesh['rows_0'=2,'rows_1'=4,'cols_0'=8,'cols_1'=2,'cols_2'=2] {'cols_2'}, use_global_device_ids=true, to_apply=%region_47.0 | all-reduce | flops 512 | bytes 4096 | tf_op jit(solution)/shard_map/psum | solution.py:18
  311.4 1.6 multiply_convert_fusion.1
  314.9 2.9 add_convert_fusion
  318.3 2.0 copy.138
  320.3 236.9 %all-reduce.22.cloned.1.call-done = f32[72192]{0:T(1024)} async-done(((f32[72192]{0:T(1024)}), f32[72192]{0:T(1024)}) %all-reduce.22.cloned.1.call-update) | async-done | bytes 288784 | tf_op jit(solution)/shard_map/psum | solution.py:40
  (180 shorter events, 43.5 us)
Async XLA Ops:
  7.2 2.9 copy-start.36
  7.2 2.9 copy-start.35
  7.2 550.0 %all-reduce.22.cloned.1.call-start = ((), (), s32[]{:S(2)}) async-start(), calls=%async_computation | async-start | bytes 581632 | tf_op jit(solution)/shard_map/psum | solution.py:40
  10.1 0.6 copy-start.29
  10.1 46.3 %copy-start.39 = (f32[64]{0:T(128)S(1)}, f32[64]{0:T(128)}, u32[]{:S(2)}) copy-start(f32[64]{0:T(128)} %param.22) | copy-start | bytes 772
  10.1 46.3 %copy-start.42 = (f32[64]{0:T(128)S(1)}, f32[64]{0:T(128)}, u32[]{:S(2)}) copy-start(f32[64]{0:T(128)} %param.23) | copy-start | bytes 772
  10.7 47.4 %copy-start = (f32[4,64,1024]{2,1,0:T(8,128)}, f32[4,64,1024]{2,1,0:T(8,128)S(1)}, u32[]{:S(2)}) copy-start(f32[4,64,1024]{2,1,0:T(8,128)S(1)} %get-tuple-element.147) | copy-start | bytes 3145732
  57.2 1.0 copy-start.2
  58.2 6.9 %copy-start.38 = (f32[4,64]{1,0:T(4,128)S(1)}, f32[4,64]{1,0:T(4,128)}, u32[]{:S(2)}) copy-start(f32[4,64]{1,0:T(4,128)} %param.19) | copy-start | bytes 3076
  60.0 6.0 %copy-start.37 = (bf16[64,256]{1,0:T(8,128)(2,1)S(1)}, bf16[64,256]{1,0:T(8,128)(2,1)}, u32[]{:S(2)}) copy-start(bf16[64,256]{1,0:T(8,128)(2,1)} %param.17) | copy-start | bytes 98308
  60.8 10.4 %collective-permute-start = (bf16[4,64,1,128]{1,0,3,2:T(4,128)(2,1)}, bf16[4,64,1,128]{1,0,3,2:T(4,128)(2,1)}, u32[]{:S(2)}, u32[]{:S(2)}) collective-permute-start(bf16[4,64,1,128]{1,0,3,2:T(4,128)(2,1)} %get-tuple-element.125), channel_id=1, source_target_pairs={{0,32},{32,64},{64,96},{96,128},{128,160},{160,192},{192,224},{1,3... | collective-permute-start | bytes 196616 | tf_op jit(solution)/shard_map/ppermute | solution.py:29
  62.8 8.5 %collective-permute-start.1 = (bf16[4,64,1,128]{1,0,3,2:T(4,128)(2,1)}, bf16[4,64,1,128]{1,0,3,2:T(4,128)(2,1)}, u32[]{:S(2)}, u32[]{:S(2)}) collective-permute-start(bf16[4,64,1,128]{1,0,3,2:T(4,128)(2,1)} %get-tuple-element.126), channel_id=1, source_target_pairs={{32,0},{64,32},{96,64},{128,96},{160,128},{192,160},{224,192},{33,... | collective-permute-start | bytes 196616 | tf_op jit(solution)/shard_map/ppermute | solution.py:31
  71.9 15.9 %collective-permute-start.2 = (bf16[4,64,10,1]{1,0,3,2:T(4,128)(2,1)S(1)}, bf16[4,64,10,1]{1,0,3,2:T(4,128)(2,1)S(1)}, u32[]{:S(2)}, u32[]{:S(2)}) collective-permute-start(bf16[4,64,10,1]{1,0,3,2:T(4,128)(2,1)S(1)} %get-tuple-element.122), channel_id=1, source_target_pairs={{0,1},{1,2},{2,3},{3,4},{4,5},{5,6},{6,7},{7,8},{8,9},{9,10},{10,1... | collective-permute-start | bytes 15368 | tf_op jit(solution)/shard_map/ppermute | solution.py:29
  75.5 12.4 %collective-permute-start.3 = (bf16[4,64,10,1]{1,0,3,2:T(4,128)(2,1)S(1)}, bf16[4,64,10,1]{1,0,3,2:T(4,128)(2,1)S(1)}, u32[]{:S(2)}, u32[]{:S(2)}) collective-permute-start(bf16[4,64,10,1]{1,0,3,2:T(4,128)(2,1)S(1)} %get-tuple-element.121), channel_id=1, source_target_pairs={{1,0},{2,1},{3,2},{4,3},{5,4},{6,5},{7,6},{8,7},{9,8},{10,9},{11,1... | collective-permute-start | bytes 15368 | tf_op jit(solution)/shard_map/ppermute | solution.py:31
  98.7 4.8 copy-start.6
  98.7 4.8 copy-start.4
  103.4 1.0 copy-start.19
  104.5 1.0 copy-start.10
  105.5 1.0 copy-start.8
  106.6 1.0 copy-start.3
  115.8 1.7 copy-start.14
  117.5 1.0 copy-start.17
  118.5 1.0 copy-start.12
  119.6 46.2 %copy-start.44 = (f32[64]{0:T(128)S(1)}, f32[64]{0:T(128)}, u32[]{:S(2)}) copy-start(f32[64]{0:T(128)} %param.24) | copy-start | bytes 772
  165.8 4.7 copy-start.24
  165.8 4.7 copy-start.33
  165.8 4.7 copy-start.45
  165.8 4.7 copy-start.46
  165.8 4.7 copy-start.47
  165.9 4.7 copy-start.48
  170.6 2.0 copy-start.23
  214.4 3.2 copy-start.7
  217.6 1.7 copy-start.20
  217.9 1.7 copy-start.11
  219.2 1.0 copy-start.9
  220.3 1.0 copy-start.16
  220.6 1.1 copy-start.15
  221.3 1.1 copy-start.18
  221.7 1.1 copy-start.13
  223.0 1.2 copy-start.28
  226.1 8.8 %copy-start.34 = (f32[64,256]{1,0:T(8,128)S(1)}, f32[64,256]{1,0:T(8,128)}, u32[]{:S(2)}) copy-start(f32[64,256]{1,0:T(8,128)} %get-tuple-element.60) | copy-start | bytes 196612
  226.9 10.6 %collective-permute-start.4 = (bf16[4,64,1,128]{1,0,3,2:T(4,128)(2,1)}, bf16[4,64,1,128]{1,0,3,2:T(4,128)(2,1)}, u32[]{:S(2)}, u32[]{:S(2)}) collective-permute-start(bf16[4,64,1,128]{1,0,3,2:T(4,128)(2,1)} %get-tuple-element.123), channel_id=1, source_target_pairs={{0,32},{32,64},{64,96},{96,128},{128,160},{160,192},{192,224},{1,3... | collective-permute-start | bytes 196616 | tf_op jit(solution)/shard_map/ppermute | solution.py:29
  231.2 5.7 copy-start.41
  231.2 6.8 %collective-permute-start.5 = (bf16[4,64,1,128]{1,0,3,2:T(4,128)(2,1)}, bf16[4,64,1,128]{1,0,3,2:T(4,128)(2,1)}, u32[]{:S(2)}, u32[]{:S(2)}) collective-permute-start(bf16[4,64,1,128]{1,0,3,2:T(4,128)(2,1)} %get-tuple-element.124), channel_id=1, source_target_pairs={{32,0},{64,32},{96,64},{128,96},{160,128},{192,160},{224,192},{33,... | collective-permute-start | bytes 196616 | tf_op jit(solution)/shard_map/ppermute | solution.py:31
  238.7 15.0 %collective-permute-start.6 = (bf16[4,64,10,1]{1,0,3,2:T(4,128)(2,1)S(1)}, bf16[4,64,10,1]{1,0,3,2:T(4,128)(2,1)S(1)}, u32[]{:S(2)}, u32[]{:S(2)}) collective-permute-start(bf16[4,64,10,1]{1,0,3,2:T(4,128)(2,1)S(1)} %get-tuple-element.118), channel_id=1, source_target_pairs={{1,0},{2,1},{3,2},{4,3},{5,4},{6,5},{7,6},{8,7},{9,8},{10,9},{11,1... | collective-permute-start | bytes 15368 | tf_op jit(solution)/shard_map/ppermute | solution.py:31
  242.1 11.6 %collective-permute-start.7 = (bf16[4,64,10,1]{1,0,3,2:T(4,128)(2,1)S(1)}, bf16[4,64,10,1]{1,0,3,2:T(4,128)(2,1)S(1)}, u32[]{:S(2)}, u32[]{:S(2)}) collective-permute-start(bf16[4,64,10,1]{1,0,3,2:T(4,128)(2,1)S(1)} %get-tuple-element.117), channel_id=1, source_target_pairs={{0,1},{1,2},{2,3},{3,4},{4,5},{5,6},{6,7},{7,8},{8,9},{9,10},{10,1... | collective-permute-start | bytes 15368 | tf_op jit(solution)/shard_map/ppermute | solution.py:29
  258.9 1.4 copy-start.5
  260.8 1.2 copy-start.27
  262.3 1.2 copy-start.25
  264.7 1.0 copy-start.26
  265.7 1.2 copy-start.1
  265.7 1.2 copy-start.40
  265.7 1.2 copy-start.43
  310.8 2.1 copy-start.30
  312.9 0.8 copy-start.21
  312.9 1.1 copy-start.31
  313.8 1.1 copy-start.22
  314.1 0.7 copy-start.32
Sparse Core Ops, SparseCore 0:
  315.0 242.1 all-reduce.21
where the time goes:
time: 575 us; the launch traced here: 572 us
  waiting for transfers between devices  237 us (41%)
  blocking collectives  172 us (30%)
  local copies, waits for them, and re-layouts  71 us (12%)
  other arithmetic  28.2 us (5%)
  matrix products  28 us (5%)
  starting transfers between devices  20.1 us (3%)
  between operations  14.9 us (3%)
    psum x1, waiting for transfers between devices, packed_total(): so_far = lax.psum(flat, axis)  237 us
    psum x20, blocking collectives, by_axis(): return functools.reduce(lax.psum, axes, array)  172 us
    reshape x8, local copies, waits for them, and re-layouts, conv_forward(): padded[:, :, row_off:row_off + tall, col_off:col_off + broad]  17.3 us
    concatenate x6, other arithmetic, with_halo(): jnp.concatenate([lax.ppermute(tail, axis, [(i, (i + 1) % count) for i in...  17.3 us
    unnamed x111, local copies, waits for them, and re-layouts  13.8 us
    ppermute x4, starting transfers between devices, with_halo(): lax.ppermute(tail, axis, [(i, (i + 1) % count) for i in range(ends)])  12.1 us
  transfers between devices with their start and end apart: 9, of which 2 were waited for; matrix products, arithmetic and copies ran while one was open for 6% of the time, Pallas kernels for 0%

commit v1 on v0

v1 whole, which is shorter than its diff:
```python
import functools

import jax
import jax.numpy as jnp
from jax import lax
from jax.experimental import pallas as pl
from jax.experimental.pallas import tpu as pltpu
from jax.sharding import Mesh
from jax.sharding import PartitionSpec as P

ROWS = ("rows_0", "rows_1")
COLS = ("cols_0", "cols_1", "cols_2")
MESH = pl.DeviceIdType.MESH
EPSILON = 1e-05
F32 = jnp.float32
BF16 = jnp.bfloat16

CHUNK = 40
EXPAND, REDUCE, SPATIAL, REDUCE_F, OUTPUT_F, COLUMN_F = 0, 128, 256, 544, 552, 560


def dot(a, b, ca, cb):
    return lax.dot_general(a, b, (((ca,), (cb,)), ((), ())), preferred_element_type=F32)


def sigmoid(v):
    return 1.0 / (1.0 + jnp.exp(-v))


def silu(v):
    return v * sigmoid(v)


def slope(v):
    s = sigmoid(v)
    return s * (1.0 + v * (1.0 - s))


def lanes(shape):
    return lax.broadcasted_iota(jnp.int32, shape, len(shape) - 1)


def kernel(
    x_hbm, c_hbm, w1, w2, w2b, w3, rwt, sw, ew, rf, of, sfc, efc, gb,
    out_hbm, o_reduce, o_spatial, o_expand, o_rf, o_sf, o_ef, o_of, o_norm,
    x, c, u, hb, hq, dq, dpre1, nf, pk, pr, arb, ara, g, r1, r2, r3, cols,
    ld_sem, st_sem, s_sem, r_sem, hs_sem, hr_sem,
):
    count = float(64 * 4096)
    x_hi, y = lax.axis_index("rows_0"), lax.axis_index("rows_1")
    z, x_lo, core = lax.axis_index("cols_0"), lax.axis_index("cols_1"), lax.axis_index("cols_2")
    row = x_hi * 4 + y
    col = z * 4 + x_lo * 2 + core
    rank_a = x_hi * 8 + x_lo * 4 + y
    rank_b = z * 2 + core

    def peer_a(d):
        a = lax.rem(rank_a + d, 16)
        return (a // 8, lax.rem(a, 4), z, lax.rem(a // 4, 2), core)

    def peer_b(d):
        b = lax.rem(rank_b + d, 16)
        return (x_hi, y, b // 2, x_lo, lax.rem(b, 2))

    def at(dr, dc):
        rr, cc = lax.rem(row + dr + 8, 8), lax.rem(col + dc + 32, 32)
        return (rr // 4, lax.rem(rr, 4), cc // 4, lax.rem(cc // 2, 2), lax.rem(cc, 2))

    sides = ((0, 1), (0, -1), (1, 1), (1, -1), (-1, 1), (-1, -1))

    load_x = [pltpu.make_async_copy(x_hbm.at[m], x.at[m], ld_sem.at[m]) for m in range(4)]
    load_c = [pltpu.make_async_copy(c_hbm.at[m], c.at[m], ld_sem.at[4 + m]) for m in range(4)]
    for copy in load_x + load_c:
        copy.start()

    barrier = pltpu.get_barrier_semaphore()

    def greet(d, _):
        pl.semaphore_signal(barrier, inc=1, device_id=peer_a(d), device_id_type=MESH)
        pl.semaphore_signal(barrier, inc=1, device_id=peer_b(d), device_id_type=MESH)
        return 0

    lax.fori_loop(1, 16, greet, 0)
    for side in sides:
        pl.semaphore_signal(barrier, inc=1, device_id=at(*side), device_id_type=MESH)

    def exchange(stage, src, buf, rank, peer):
        def copy(d):
            return pltpu.make_async_remote_copy(
                src_ref=src(d), dst_ref=buf.at[rank], send_sem=s_sem.at[stage, d],
                recv_sem=r_sem.at[stage, d], device_id=peer(d), device_id_type=MESH,
            )

        def start(d, _):
            copy(d).start()
            return 0

        def wait(d, _):
            copy(d).wait()
            return 0

        return (lambda: lax.fori_loop(1, 16, start, 0)), (lambda: lax.fori_loop(1, 16, wait, 0))

    def total(buf):
        t = buf[0]
        for k in range(1, 16):
            t = t + buf[k]
        return t

    def reduce_start(k, tile):
        arb[k, rank_b] = tile
        start, wait = exchange(2 * k, lambda d: arb.at[k, rank_b], arb.at[k], rank_b, peer_b)
        start()
        return wait

    def reduce_end(k, wait):
        wait()
        ara[k, rank_a] = total(arb.at[k])
        start, wait = exchange(2 * k + 1, lambda d: ara.at[k, rank_a], ara.at[k], rank_a, peer_a)
        start()
        wait()
        return total(ara.at[k])

    def halo(k):
        copies = [
            pltpu.make_async_remote_copy(
                src_ref=hb.at[k, :, :, pl.ds(128, 128)], dst_ref=hb.at[k, :, :, pl.ds(1152, 128)],
                send_sem=hs_sem.at[k, 6], recv_sem=hr_sem.at[k, 6],
                device_id=at(-1, 0), device_id_type=MESH,
            ),
            pltpu.make_async_remote_copy(
                src_ref=hb.at[k, :, :, pl.ds(1024, 128)], dst_ref=hb.at[k, :, :, pl.ds(0, 128)],
                send_sem=hs_sem.at[k, 7], recv_sem=hr_sem.at[k, 7],
                device_id=at(1, 0), device_id_type=MESH,
            ),
        ]
        for n, side in enumerate(sides):
            copies.append(
                pltpu.make_async_remote_copy(
                    src_ref=pk.at[k], dst_ref=pr.at[k, n], send_sem=hs_sem.at[k, n],
                    recv_sem=hr_sem.at[k, n], device_id=at(*side), device_id_type=MESH,
                )
            )
        return copies

    lane = lanes((64, 128))

    def put(acc, n, value):
        return jnp.where(lane == n, value, acc)

    def rows_of_columns(acc):
        return jnp.transpose(jnp.concatenate([acc, jnp.zeros((64, 128), F32)], axis=0))[:8]

    def columns_of_rows(tile, k):
        t = jnp.transpose(jnp.concatenate([tile, jnp.zeros((120, 128), F32)], axis=0))
        for m in range(4):
            cols[k, m] = t[:64, m : m + 1]
            cols[k + 1, m] = t[:64, 4 + m : 5 + m]

    def sums(m, acc, a, b):
        acc = put(acc, m, jnp.sum(a, axis=1, keepdims=True))
        return put(acc, 4 + m, jnp.sum(b, axis=1, keepdims=True))

    def pack(k, m, acc):
        for i in range(8):
            t = hb[k, m, :, 128 + i * 128 : 256 + i * 128]
            acc = put(acc, m * 8 + i, t[:, 0:1])
            acc = put(acc, 32 + m * 8 + i, t[:, 127:128])
        return acc

    top = jnp.where(row > 0, 1.0, 0.0).astype(F32)
    bottom = jnp.where(row < 7, 1.0, 0.0).astype(F32)
    left = jnp.where(col > 0, 1.0, 0.0).astype(F32)
    right = jnp.where(col < 31, 1.0, 0.0).astype(F32)
    masks = (left, right, top * left, top * right, bottom * left, bottom * right)

    def spread(dst, m, tile, edge):
        edges = [edge(n) * masks[n] for n in range(6)]
        for i in range(10):
            t = tile(i)
            if i == 0:
                t, e0, e2, at_row = t * top, edges[2], edges[3], 7
            elif i == 9:
                t, e0, e2, at_row = t * bottom, edges[4], edges[5], 0
            else:
                e0, e2, at_row = edges[0], edges[1], i - 1
            where0 = 32 + m * 8 + at_row
            where2 = m * 8 + at_row
            before = jnp.where(
                lane == 0, pltpu.roll(e0, 128 - where0, axis=1), pltpu.roll(t, 1, axis=1)
            )
            after = jnp.where(
                lane == 127, pltpu.roll(e2, 127 - where2, axis=1), pltpu.roll(t, 127, axis=1)
            )
            span = slice(i * 128, i * 128 + 128)
            dst[m, 0:64, span] = before.astype(BF16)
            dst[m, 64:128, span] = t.astype(BF16)
            dst[m, 128:192, span] = after.astype(BF16)

    zero = jnp.zeros((64, 128), F32)

    def first_of(m, carry):
        acc, edge = carry
        a = dot(w1[m], x[m], 1, 0)
        hb[0, m, :, 128:1152] = a
        return sums(m, acc, a, a * a), pack(0, m, edge)

    for copy in load_x:
        copy.wait()
    acc, edge = lax.fori_loop(0, 4, first_of, (zero, zero))
    pk[0] = edge
    pl.semaphore_wait(barrier, 36)
    wait = reduce_start(0, rows_of_columns(acc))
    halos = halo(0)
    for copy in halos:
        copy.start()
    stats = reduce_end(0, wait)
    for copy in halos:
        copy.wait()

    def moments(k, tile):
        columns_of_rows(tile, k)
        for m in range(4):
            mean = cols[k, m] / count
            var = cols[k + 1, m] / count - mean * mean
            cols[k, m] = mean
            cols[k + 1, m] = lax.rsqrt(var + EPSILON)

    moments(0, stats)
    gain1, shift1, gain2, shift2 = (gb[n] for n in range(4))

    def second_of(m, carry):
        acc, edge = carry
        mean, rstd = cols[0, m], cols[1, m]

        def hidden(v):
            return silu(gain1 * ((v - mean) * rstd) + shift1)

        spread(
            hq, m, lambda i: hidden(hb[0, m, :, i * 128 : i * 128 + 128]),
            lambda n: hidden(pr[0, n]),
        )
        a = dot(w2[m, 0], hq[m, :, 0:1024], 0, 0)
        a = a + dot(w2[m, 1], hq[m, :, 128:1152], 0, 0)
        a = a + dot(w2[m, 2], hq[m, :, 256:1280], 0, 0)
        hb[1, m, :, 128:1152] = a
        return sums(m, acc, a, a * a), pack(1, m, edge)

    acc, edge = lax.fori_loop(0, 4, second_of, (zero, zero))
    pk[1] = edge
    wait = reduce_start(1, rows_of_columns(acc))
    halos = halo(1)
    for copy in halos:
        copy.start()
    stats = reduce_end(1, wait)
    for copy in halos:
        copy.wait()
    moments(2, stats)
    for copy in load_c:
        copy.wait()

    g[EXPAND : EXPAND + 128] = jnp.zeros((128, 128), F32)
    g[REDUCE : REDUCE + 128] = jnp.zeros((128, 128), F32)
    g[568:640] = jnp.zeros((72, 128), F32)

    def upstream_of(m, carry):
        acc, edge, fac = carry
        mean, rstd = cols[2, m], cols[3, m]

        def chunk(j, sums_):
            plain, weighted, part = sums_
            o = pl.multiple_of(j * 256, 256)
            normed = (hb[1, m, :, pl.ds(o + 128, 256)] - mean) * rstd
            pre = gain2 * normed + shift2
            s = sigmoid(pre)
            low = (pre * s).astype(BF16)
            third = dot(w3[m], low, 0, 0)
            up = c[m, :, pl.ds(o, 256)].astype(F32) * slope(x[m, :, pl.ds(o, 256)].astype(F32) + third)
            u[m, :, pl.ds(o, 256)] = up
            up = up.astype(BF16)
            back = dot(w3[m], up, 1, 0)
            hb[2, m, :, pl.ds(o + 128, 256)] = back
            dpre = back * (s * (1.0 + pre * (1.0 - s)))
            part = part + dot(low, up, 1, 1)
            plain = plain + jnp.sum(dpre, axis=1, keepdims=True)
            weighted = weighted + jnp.sum(dpre * normed, axis=1, keepdims=True)
            return plain, weighted, part

        one = jnp.zeros((64, 1), F32)
        plain, weighted, part = lax.fori_loop(0, 4, chunk, (one, one, jnp.zeros((64, 256), F32)))
        acc = put(put(acc, m, plain), 4 + m, weighted)
        ofm = of[m]
        ef = efc[m]
        scaled = part * ef * ofm
        g[EXPAND : EXPAND + 64] += scaled[:, :128]
        g[EXPAND + 64 : EXPAND + 128] += scaled[:, 128:]
        byw = part * ew[...]
        fac = put(fac, m, jnp.sum(byw * ofm, axis=1, keepdims=True))
        nf[1, m] = jnp.sum(byw * ef, axis=0, keepdims=True)
        return acc, pack(2, m, edge), fac

    acc, edge, fac = lax.fori_loop(0, 4, upstream_of, (zero, zero, zero))
    pk[2] = edge
    wait = reduce_start(2, rows_of_columns(acc))
    halos = halo(2)
    for copy in halos:
        copy.start()
    stats2 = reduce_end(2, wait)
    for copy in halos:
        copy.wait()
    columns_of_rows(stats2, 4)

    def back_of(m, carry):
        acc, fac = carry
        mean, rstd, plain, weighted = cols[2, m], cols[3, m], cols[4, m] / count, cols[5, m] / count

        def dact(second, back):
            normed = (second - mean) * rstd
            dpre = back * slope(gain2 * normed + shift2)
            return gain2 * rstd * (dpre - plain - normed * weighted)

        spread(
            dq, m,
            lambda i: dact(hb[1, m, :, i * 128 : i * 128 + 128], hb[2, m, :, i * 128 : i * 128 + 128]),
            lambda n: dact(pr[1, n], pr[2, n]),
        )
        a = dot(w2b[m, 0], dq[m, :, 0:1024], 1, 0)
        a = a + dot(w2b[m, 1], dq[m, :, 128:1152], 1, 0)
        a = a + dot(w2b[m, 2], dq[m, :, 256:1280], 1, 0)
        normed = (hb[0, m, :, 128:1152] - cols[0, m]) * cols[1, m]
        dpre = a * slope(gain1 * normed + shift1)
        dpre1[m] = dpre
        acc = sums(m, acc, dpre, dpre * normed)

        low = dq[m, 64:128, 128:1152]
        sf = sfc[m]
        byf = jnp.zeros((64, 1), F32)
        halves = []
        for p in range(3):
            part = dot(hq[m, :, p * 128 : p * 128 + 1024], low, 1, 1)
            byw = jnp.sum(part * sw[p * 192 : p * 192 + 192], axis=1, keepdims=True)
            byf = byf + byw[0:64] + byw[64:128] + byw[128:192]
            for q in range(3):
                halves.append(part[q * 64 : q * 64 + 64] * sf)
        whole = jnp.concatenate(halves, axis=0)
        whole = jnp.concatenate([whole[:288], whole[288:]], axis=1)

        @pl.when(m == 0)
        def _():
            g[SPATIAL : SPATIAL + 288] = whole

        @pl.when(m > 0)
        def _():
            g[SPATIAL : SPATIAL + 288] += whole

        return acc, put(fac, 4 + m, byf)

    acc, fac = lax.fori_loop(0, 4, back_of, (zero, fac))
    wait = reduce_start(3, rows_of_columns(acc))
    g[COLUMN_F : COLUMN_F + 8] = rows_of_columns(fac)
    stats1 = reduce_end(3, wait)
    columns_of_rows(stats1, 6)

    def low_of(m, _):
        mean, rstd, plain, weighted = cols[0, m], cols[1, m], cols[6, m] / count, cols[7, m] / count
        normed = (hb[0, m, :, 128:1152] - mean) * rstd
        d = (gain1 * rstd * (dpre1[m] - plain - normed * weighted)).astype(BF16)
        dq[m, 0:64, 0:1024] = d
        part = dot(d, x[m], 1, 1)
        scaled = part * rf[m]
        g[REDUCE : REDUCE + 64] += scaled[:, :128]
        g[REDUCE + 64 : REDUCE + 128] += scaled[:, 128:]
        nf[0, m] = jnp.sum(part * rwt[...], axis=0, keepdims=True)
        return 0

    lax.fori_loop(0, 4, low_of, 0)
    for k, at_row in ((0, REDUCE_F), (1, OUTPUT_F)):
        g[at_row : at_row + 8] = jnp.concatenate(
            [nf[k, m, :, h * 128 : h * 128 + 128] for h in range(2) for m in range(4)], axis=0
        )

    def chunk_of(d):
        return g.at[pl.ds(pl.multiple_of(lax.rem(rank_a + d, 16) * CHUNK, 8), CHUNK)]

    start, wait = exchange(8, chunk_of, r1, rank_a, peer_a)
    start()

    def grad_of(m, _):
        def chunk(j, _):
            o = pl.multiple_of(j * 256, 256)
            t = dot(w1[m], dq[m, 0:64, pl.ds(o, 256)], 0, 0)
            c[m, :, pl.ds(o, 256)] = (u[m, :, pl.ds(o, 256)] + t).astype(BF16)
            return 0

        lax.fori_loop(0, 4, chunk, 0)
        return 0

    lax.fori_loop(0, 4, grad_of, 0)
    stores = [pltpu.make_async_copy(c.at[m], out_hbm.at[m], st_sem.at[m]) for m in range(4)]
    for copy in stores:
        copy.start()

    wait()
    r1[rank_a] = g[pl.ds(pl.multiple_of(rank_a * CHUNK, 8), CHUNK)]
    r2[rank_b] = total(r1)
    start, wait = exchange(9, lambda d: r2.at[rank_b], r2, rank_b, peer_b)
    start()
    wait()
    r3[rank_a] = total(r2)
    start, wait = exchange(10, lambda d: r3.at[rank_a], r3, rank_a, peer_a)
    start()
    wait()

    def rows(at_row, n):
        return jnp.concatenate(
            [r3[r // CHUNK, r % CHUNK : r % CHUNK + 8] for r in range(at_row, at_row + n, 8)], axis=0
        )

    e = rows(EXPAND, 128)
    o_expand[...] = jnp.concatenate([e[:64], e[64:]], axis=1)
    e = rows(REDUCE, 128)
    o_reduce[...] = jnp.transpose(jnp.concatenate([e[:64], e[64:]], axis=1))
    e = rows(SPATIAL, 288)
    o_spatial[0:288] = e[:, :64]
    o_spatial[288:576] = e[:, 64:]
    e = rows(REDUCE_F, 8)
    o_rf[...] = jnp.concatenate([e[:4], e[4:]], axis=1)
    e = rows(OUTPUT_F, 8)
    o_of[...] = jnp.concatenate([e[:4], e[4:]], axis=1)
    e = rows(COLUMN_F, 8)
    o_ef[...] = e[:4, :64]
    o_sf[...] = e[4:, :64]
    o_norm[...] = jnp.concatenate(
        [
            jnp.sum(stats1[4:8], axis=0, keepdims=True),
            jnp.sum(stats1[0:4], axis=0, keepdims=True),
            jnp.sum(stats2[4:8], axis=0, keepdims=True),
            jnp.sum(stats2[0:4], axis=0, keepdims=True),
        ],
        axis=0,
    )[:, :64]
    for copy in stores:
        copy.wait()


def body(
    features, cotangent, reduce_weight, spatial_weight, expand_weight,
    reduce_factor, spatial_factor, expand_factor, output_factor,
    gain_first, shift_first, gain_second, shift_second,
):
    rw = reduce_weight.astype(F32)
    sw = spatial_weight.astype(F32)
    ew = expand_weight.astype(F32)
    rwt = rw.T
    w1 = (reduce_factor[:, None, :] * rwt[None]).astype(BF16)
    spatial = (spatial_factor[:, None, :, None] * sw[None]).astype(BF16)
    w2 = spatial.reshape(4, 3, 192, 64)
    w2b = spatial.reshape(4, 3, 3, 64, 64)[:, ::-1, ::-1].transpose(0, 1, 3, 2, 4).reshape(4, 3, 64, 192)
    w3 = (expand_factor[:, :, None] * ew[None] * output_factor[:, None, :]).astype(BF16)
    gb = jnp.stack([gain_first, shift_first, gain_second, shift_second])[:, :, None]
    vmem = pl.BlockSpec(memory_space=pltpu.VMEM)
    hbm = pl.BlockSpec(memory_space=pl.ANY)
    sds = jax.ShapeDtypeStruct
    outs = pl.pallas_call(
        kernel,
        out_shape=(
            sds((4, 256, 1024), BF16), sds((256, 64), F32), sds((576, 64), F32), sds((64, 256), F32),
            sds((4, 256), F32), sds((4, 64), F32), sds((4, 64), F32), sds((4, 256), F32), sds((4, 64), F32),
        ),
        in_specs=[hbm, hbm] + [vmem] * 12,
        out_specs=(hbm,) + (vmem,) * 8,
        scratch_shapes=[
            pltpu.VMEM((4, 256, 1024), BF16),
            pltpu.VMEM((4, 256, 1024), BF16),
            pltpu.VMEM((4, 256, 1024), F32),
            pltpu.VMEM((3, 4, 64, 1280), F32),
            pltpu.VMEM((4, 192, 1280), BF16),
            pltpu.VMEM((4, 192, 1280), BF16),
            pltpu.VMEM((4, 64, 1024), F32),
            pltpu.VMEM((2, 4, 1, 256), F32),
            pltpu.VMEM((3, 64, 128), F32),
            pltpu.VMEM((3, 6, 64, 128), F32),
            pltpu.VMEM((4, 16, 8, 128), F32),
            pltpu.VMEM((4, 16, 8, 128), F32),
            pltpu.VMEM((16 * CHUNK, 128), F32),
            pltpu.VMEM((16, CHUNK, 128), F32),
            pltpu.VMEM((16, CHUNK, 128), F32),
            pltpu.VMEM((16, CHUNK, 128), F32),
            pltpu.VMEM((8, 4, 64, 1), F32),
            pltpu.SemaphoreType.DMA((8,)),
            pltpu.SemaphoreType.DMA((4,)),
            pltpu.SemaphoreType.DMA((11, 16)),
            pltpu.SemaphoreType.DMA((11, 16)),
            pltpu.SemaphoreType.DMA((3, 8)),
            pltpu.SemaphoreType.DMA((3, 8)),
        ],
        compiler_params=pltpu.CompilerParams(
            collective_id=0, has_side_effects=True, vmem_limit_bytes=56 * 1024 * 1024
        ),
    )(
        features.reshape(4, 256, 1024), cotangent.reshape(4, 256, 1024), w1, w2, w2b, w3,
        rwt, sw.reshape(576, 64), ew, reduce_factor[:, None, :], output_factor[:, None, :],
        spatial_factor[:, :, None], expand_factor[:, :, None], gb,
    )
    grad, o_reduce, o_spatial, o_expand, o_rf, o_sf, o_ef, o_of, o_norm = outs
    return (
        grad.reshape(4, 256, 8, 128), o_reduce, o_spatial.reshape(9, 64, 64), o_expand,
        o_rf, o_sf, o_ef, o_of, o_norm[0], o_norm[1], o_norm[2], o_norm[3],
    )


def solution(mesh):
    split = Mesh(
        mesh.devices.reshape(2, 4, 8, 2, 2), ("rows_0", "rows_1", "cols_0", "cols_1", "cols_2")
    )
    image = P(None, None, ROWS, COLS)
    return jax.shard_map(
        body,
        mesh=split,
        in_specs=(image, image) + (P(),) * 11,
        out_specs=(image,) + (P(),) * 11,
        check_vma=False,
    )
```

time: 575 us -> 133 us (0.23)
  waiting for transfers between devices: 237 us -> 0 us
  blocking collectives: 172 us -> 0 us
  Pallas kernels: 0 us -> 102 us
  local copies, waits for them, and re-layouts: 71 us -> 23.4 us
  matrix products: 28 us -> 0 us
  other arithmetic: 28.2 us -> 5.97 us
  starting transfers between devices: 20.1 us -> 0 us
  between operations: 14.9 us -> 0.78 us
    psum x1 -> x0, waiting for transfers between devices: 237 us -> none  [packed_total(): so_far = lax.psum(flat, axis)]
    psum x20 -> x0, blocking collectives: 172 us -> none  [by_axis(): return functools.reduce(lax.psum, axes, array)]
    pallas_call x0 -> x1, Pallas kernels: none -> 102 us  [body(): pl.pallas_call(kernel, out_shape=(sds((4, 256, 1024), BF16), sds((256, 64...]
    dot_general x33 -> x0, matrix products: 28 us -> none  [the longest x9 6.61 us: conv_backward(): jnp.einsum('mfo,mop->mfp', weights[:, tap], flipped, preferred_element_ty...]
    reshape x21 -> x3, local copies, waits for them, and re-layouts: 31.3 us -> 7.61 us  [the longest x1 4.3 us: body(): features.reshape(4, 256, 1024)]
    ppermute x8 -> x0, starting transfers between devices: 20.1 us -> none  [the longest x4 12.1 us: with_halo(): lax.ppermute(tail, axis, [(i, (i + 1) % count) for i in range(ends)])]
    concatenate x6 -> x0, other arithmetic: 17.3 us -> none  [with_halo(): jnp.concatenate([lax.ppermute(tail, axis, [(i, (i + 1) % count) for i in...]
    slice x12 -> x0, local copies, waits for them, and re-layouts: 13.4 us -> none  [the longest x7 5.11 us: packed_total(): finished.append(so_far[at:at + a.size].reshape(a.shape))]
  transfers between devices with their start and end apart: 9 -> 0, of which waited for: 2 -> 0; matrix products, arithmetic and copies ran while one was open for 6% -> 0% of each run, Pallas kernels for 0% -> 0%
where the time goes in v1:
time: 133 us; the launch traced here: 132 us
  Pallas kernels  102 us (77%)
  local copies, waits for them, and re-layouts  23.4 us (18%)
  other arithmetic  5.97 us (4%)
    pallas_call x1, Pallas kernels, body(): pl.pallas_call(kernel, out_shape=(sds((4, 256, 1024), BF16), sds((256, 64...  102 us
    unnamed x34, local copies, waits for them, and re-layouts  8.06 us
    reshape x1, local copies, waits for them, and re-layouts, body(): features.reshape(4, 256, 1024)  4.3 us

profile of v1, /device:TPU:1, one launch (start us, length us, event | category | flops | bytes accessed | tf_op | source)
XLA Modules:
  0.0 132.2 jit_solution(2922032891227712510)
XLA Ops:
  0.6 0.0 copy-start.7
  0.7 0.7 maximum_bitcast_fusion
  1.4 1.3 broadcast_in_dim.10.rf
  2.7 1.3 broadcast_in_dim.11.of
  3.9 0.7 mul.66
  4.6 0.1 mul.67
  4.7 0.8 convert_bitcast_fusion.rwt
  5.5 0.0 copy-start.2
  5.5 0.8 convert_element_type.24.ew
  6.2 0.0 copy-start.3
  6.2 0.8 copy.31.gb
  7.0 1.4 %copy.29.sfc = f32[4,64,1]{2,1,0:T(8,128)} copy(f32[4,64,1]{1,0,2:T(4,128)} %bitcast.40) | data formatting | bytes 2048 | tf_op jit(solution)/shard_map/broadcast_in_dim | solution.py:503
  8.4 1.5 %copy.30.efc = f32[4,64,1]{2,1,0:T(8,128)} copy(f32[4,64,1]{1,0,2:T(4,128)} %bitcast.41) | data formatting | bytes 2048 | tf_op jit(solution)/shard_map/broadcast_in_dim | solution.py:459
  9.9 1.5 %multiply_convert_fusion.2 = (bf16[4,64,256]{2,1,0:T(8,128)(2,1)}, bf16[4,64,256]{2,1,0:T(8,128)(2,1)}) fusion(f32[4,256]{1,0:T(4,128)} %param.21, f32[64,256]{1,0:T(8,128)S(1)} %convert_element_type.24.ew, f32[4,64]{1,0:T(4,128)} %param.20, f32[64,256]{1,0:T(8,128)S(1)} %convert_bitcast_fusion.rwt, f32[4,256]{1,0:T(4,128)} %param.18), kind=kLoop, calls=%fused_computation.2 | loop fusion | flops 327680 | bytes 402432 | tf_op jit(solution)/shard_map/convert_element_type | solution.py:459
  11.4 0.9 convert_element_type.21
  12.3 0.0 copy-start
  12.3 0.1 copy.27
  12.5 0.0 copy-done.7
  12.5 0.1 multiply_convert_fusion
  12.7 1.0 copy.28.w2b
  13.7 0.0 copy-done.2
  13.7 0.0 copy-done.3
  13.7 1.2 multiply_convert_fusion.1.w2
  14.9 0.0 copy-done
  14.9 0.0 copy-start.1
  14.9 4.3 %reshape.55.x_hbm = bf16[4,256,1024]{2,1,0:T(8,128)(2,1)} reshape(bf16[4,256,8,128]{3,2,1,0:T(8,128)(2,1)} %param.13) | data formatting | bytes 4194304 | tf_op jit(solution)/shard_map/reshape | solution.py:501
  19.2 0.0 copy-done.1
  19.2 2.3 %reshape.56.c_hbm = bf16[4,256,1024]{2,1,0:T(8,128)(2,1)} reshape(bf16[4,256,8,128]{3,2,1,0:T(8,128)(2,1)S(1)} %copy-done.1) | data formatting | bytes 4194304 | tf_op jit(solution)/shard_map/reshape | solution.py:501
  21.5 102.1 %shard_map.220 = (bf16[4,256,1024]{2,1,0:T(8,128)(2,1)}, f32[256,64]{1,0:T(8,128)}, f32[576,64]{1,0:T(8,128)}, f32[64,256]{1,0:T(8,128)}, f32[4,256]{1,0:T(4,128...) custom-call(bf16[4,256,1024]{2,1,0:T(8,128)(2,1)} %reshape.55.x_hbm, ...), custom_call_target="tpu_custom_call" | custom-call | tf_op jit(solution)/shard_map/pallas_call | solution.py:464
  123.6 0.0 copy-start.12
  123.6 0.0 copy-start.5
  123.6 0.0 copy-start.4
  123.6 0.0 copy-start.6
  123.6 0.0 copy-start.9
  123.6 0.0 copy-start.11
  123.7 0.0 copy-start.10
  123.7 0.0 copy-start.8
  123.7 3.6 %copy.33 = bf16[128,8,8,128]{3,2,1,0:T(8,128)(2,1)} copy(bf16[128,8,8,128]{3,1,2,0:T(8,128)(2,1)} %bitcast.38) | data formatting | bytes 4194304
  127.3 0.0 copy-done.12
  127.3 0.5 slice_bitcast_fusion
  127.8 0.0 copy-done.5
  127.8 0.7 copy.32
  128.5 0.0 copy-done.4
  128.5 0.7 copy.40
  129.2 0.0 copy-done.6
  129.2 0.6 copy.41
  129.9 0.0 copy-done.9
  129.9 0.6 copy.42
  130.5 0.0 copy-done.11
  130.5 0.6 copy.43
  131.1 0.0 copy-done.10
  131.1 0.6 copy.44
  131.6 0.0 copy-done.8
  131.6 0.6 copy.45
  (1 shorter events, 0.0 us)
Async XLA Ops:
  0.6 11.8 %copy-start.7 = (f32[4,64]{1,0:T(4,128)S(1)}, f32[4,64]{1,0:T(4,128)}, u32[]{:S(2)}) copy-start(f32[4,64]{1,0:T(4,128)} %param.19) | copy-start | bytes 3076
  5.5 8.2 %copy-start.2 = (f32[64,256]{1,0:T(8,128)}, f32[64,256]{1,0:T(8,128)S(1)}, u32[]{:S(2)}) copy-start(f32[64,256]{1,0:T(8,128)S(1)} %convert_bitcast_fusion.rwt) | copy-start | bytes 196612
  6.2 7.5 %copy-start.3 = (f32[64,256]{1,0:T(8,128)}, f32[64,256]{1,0:T(8,128)S(1)}, u32[]{:S(2)}) copy-start(f32[64,256]{1,0:T(8,128)S(1)} %convert_element_type.24.ew) | copy-start | bytes 196612
  12.3 2.6 %copy-start = (f32[9,64,64]{2,1,0:T(8,128)}, f32[9,64,64]{2,1,0:T(8,128)S(1)}, u32[]{:S(2)}) copy-start(f32[9,64,64]{2,1,0:T(8,128)S(1)} %convert_element_type.21) | copy-start | bytes 442372
  14.9 4.3 %copy-start.1 = (bf16[4,256,8,128]{3,2,1,0:T(8,128)(2,1)S(1)}, bf16[4,256,8,128]{3,2,1,0:T(8,128)(2,1)}, u32[]{:S(2)}) copy-start(bf16[4,256,8,128]{3,2,1,0:T(8,128)(2,1)} %param.14) | copy-start | bytes 6291460
  123.6 3.7 %copy-start.12 = (f32[4,64]{1,0:T(4,128)S(1)}, f32[4,64]{1,0:T(4,128)}, u32[]{:S(2)}) copy-start(f32[4,64]{1,0:T(4,128)} %get-tuple-element.29) | copy-start | bytes 3076
  123.6 4.2 %copy-start.5 = (f32[256,64]{1,0:T(8,128)S(1)}, f32[256,64]{1,0:T(8,128)}, u32[]{:S(2)}) copy-start(f32[256,64]{1,0:T(8,128)} %get-tuple-element.43) | copy-start | bytes 196612
  123.6 4.9 %copy-start.4 = (f32[576,64]{1,0:T(8,128)S(1)}, f32[576,64]{1,0:T(8,128)}, u32[]{:S(2)}) copy-start(f32[576,64]{1,0:T(8,128)} %get-tuple-element.23) | copy-start | bytes 442372
  123.6 5.6 %copy-start.6 = (f32[64,256]{1,0:T(8,128)S(1)}, f32[64,256]{1,0:T(8,128)}, u32[]{:S(2)}) copy-start(f32[64,256]{1,0:T(8,128)} %get-tuple-element.75) | copy-start | bytes 196612
  123.6 6.2 %copy-start.9 = (f32[4,256]{1,0:T(4,128)S(1)}, f32[4,256]{1,0:T(4,128)}, u32[]{:S(2)}) copy-start(f32[4,256]{1,0:T(4,128)} %get-tuple-element.76) | copy-start | bytes 12292
  123.6 6.8 %copy-start.11 = (f32[4,64]{1,0:T(4,128)S(1)}, f32[4,64]{1,0:T(4,128)}, u32[]{:S(2)}) copy-start(f32[4,64]{1,0:T(4,128)} %get-tuple-element.77) | copy-start | bytes 3076
  123.7 7.4 %copy-start.10 = (f32[4,64]{1,0:T(4,128)S(1)}, f32[4,64]{1,0:T(4,128)}, u32[]{:S(2)}) copy-start(f32[4,64]{1,0:T(4,128)} %get-tuple-element.78) | copy-start | bytes 3076
  123.7 8.0 %copy-start.8 = (f32[4,256]{1,0:T(4,128)S(1)}, f32[4,256]{1,0:T(4,128)}, u32[]{:S(2)}) copy-start(f32[4,256]{1,0:T(4,128)} %get-tuple-element.79) | copy-start | bytes 12292

commit v2 on v1

--- a/solution.py
+++ b/solution.py
@@ -16,7 +16,7 @@
 BF16 = jnp.bfloat16
 
 CHUNK = 40
-EXPAND, REDUCE, SPATIAL, REDUCE_F, OUTPUT_F, COLUMN_F = 0, 128, 256, 544, 552, 560
+EXPAND, REDUCE, SPATIAL, REDUCE_F, OUTPUT_F, COLUMN_F, NORMS = 0, 128, 256, 544, 552, 560, 568
 
 
 def dot(a, b, ca, cb):
@@ -41,8 +41,10 @@
 
 
 def kernel(
-    x_hbm, c_hbm, w1, w2, w2b, w3, rwt, sw, ew, rf, of, sfc, efc, gb,
-    out_hbm, o_reduce, o_spatial, o_expand, o_rf, o_sf, o_ef, o_of, o_norm,
+    x_hbm, c_hbm, rw_hbm, sw_hbm, ew_hbm, rf_hbm, sf_hbm, ef_hbm, of_hbm, g1_hbm, b1_hbm, g2_hbm, b2_hbm,
+    y_hbm, packed,
+    xraw, craw, wide, rw, sw, ew, rf, sf, ef, of, g1, b1, g2, b2,
+    w1, w2, w2b, w3, rwt,
     x, c, u, hb, hq, dq, dpre1, nf, pk, pr, arb, ara, g, r1, r2, r3, cols,
     ld_sem, st_sem, s_sem, r_sem, hs_sem, hr_sem,
 ):
@@ -68,9 +70,14 @@
 
     sides = ((0, 1), (0, -1), (1, 1), (1, -1), (-1, 1), (-1, -1))
 
-    load_x = [pltpu.make_async_copy(x_hbm.at[m], x.at[m], ld_sem.at[m]) for m in range(4)]
-    load_c = [pltpu.make_async_copy(c_hbm.at[m], c.at[m], ld_sem.at[4 + m]) for m in range(4)]
-    for copy in load_x + load_c:
+    pairs = (
+        (rw_hbm, rw), (rf_hbm, rf), (sw_hbm, sw), (ew_hbm, ew), (sf_hbm, sf), (ef_hbm, ef), (of_hbm, of),
+        (g1_hbm, g1), (b1_hbm, b1), (g2_hbm, g2), (b2_hbm, b2),
+    )
+    load_w = [pltpu.make_async_copy(a, b, ld_sem.at[8 + n]) for n, (a, b) in enumerate(pairs)]
+    load_x = [pltpu.make_async_copy(x_hbm.at[m], xraw.at[m], ld_sem.at[m]) for m in range(4)]
+    load_c = [pltpu.make_async_copy(c_hbm.at[m], craw.at[m], ld_sem.at[4 + m]) for m in range(4)]
+    for copy in load_w[:2] + load_x + load_w[2:] + load_c:
         copy.start()
 
     barrier = pltpu.get_barrier_semaphore()
@@ -199,12 +206,23 @@
 
     zero = jnp.zeros((64, 128), F32)
 
+    def flatten(src, dst, m):
+        wide[...] = src[m].astype(F32).reshape(2048, 128)
+        for i in range(8):
+            dst[m, :, i * 128 : i * 128 + 128] = wide[pl.ds(i, 256, stride=8), :].astype(BF16)
+
     def first_of(m, carry):
         acc, edge = carry
+        flatten(xraw, x, m)
         a = dot(w1[m], x[m], 1, 0)
         hb[0, m, :, 128:1152] = a
         return sums(m, acc, a, a * a), pack(0, m, edge)
 
+    for copy in load_w[:2]:
+        copy.wait()
+    rwt[...] = rw[...].astype(F32)
+    for m in range(4):
+        w1[m] = (rwt[...] * rf[m : m + 1]).astype(BF16)
     for copy in load_x:
         copy.wait()
     acc, edge = lax.fori_loop(0, 4, first_of, (zero, zero))
@@ -214,6 +232,35 @@
     halos = halo(0)
     for copy in halos:
         copy.start()
+    for copy in load_w[2:]:
+        copy.wait()
+    lines = jnp.zeros((4, 64), F32)
+    columns_of_rows(
+        jnp.concatenate(
+            [jnp.concatenate([sf[...], ef[...]], axis=0), jnp.zeros((8, 64), F32)], axis=1
+        ), 8,
+    )
+    columns_of_rows(
+        jnp.concatenate(
+            [jnp.concatenate([g1[...], b1[...], g2[...], b2[...], lines], axis=0), jnp.zeros((8, 64), F32)], axis=1
+        ), 10,
+    )
+    for m in range(4):
+        sfm, efm = cols[8, m], cols[9, m]
+        w3[m] = (efm * ew[...].astype(F32) * of[m : m + 1]).astype(BF16)
+        for p in range(3):
+            taps = [(sfm * sw[3 * p + q].astype(F32)).astype(BF16) for q in range(3)]
+            for q in range(3):
+                w2[m, p, q * 64 : q * 64 + 64] = taps[q]
+            w2b[m, 2 - p] = jnp.concatenate(taps[::-1], axis=1)
+    for copy in load_c:
+        copy.wait()
+
+    def flatten_c(m, _):
+        flatten(craw, c, m)
+        return 0
+
+    lax.fori_loop(0, 4, flatten_c, 0)
     stats = reduce_end(0, wait)
     for copy in halos:
         copy.wait()
@@ -227,7 +274,7 @@
             cols[k + 1, m] = lax.rsqrt(var + EPSILON)
 
     moments(0, stats)
-    gain1, shift1, gain2, shift2 = (gb[n] for n in range(4))
+    gain1, shift1, gain2, shift2 = (cols[10, n] for n in range(4))
 
     def second_of(m, carry):
         acc, edge = carry
@@ -256,8 +303,6 @@
     for copy in halos:
         copy.wait()
     moments(2, stats)
-    for copy in load_c:
-        copy.wait()
 
     g[EXPAND : EXPAND + 128] = jnp.zeros((128, 128), F32)
     g[REDUCE : REDUCE + 128] = jnp.zeros((128, 128), F32)
@@ -289,14 +334,14 @@
         one = jnp.zeros((64, 1), F32)
         plain, weighted, part = lax.fori_loop(0, 4, chunk, (one, one, jnp.zeros((64, 256), F32)))
         acc = put(put(acc, m, plain), 4 + m, weighted)
-        ofm = of[m]
-        ef = efc[m]
-        scaled = part * ef * ofm
+        ofm = of[pl.ds(m, 1), :]
+        efm = cols[9, m]
+        scaled = part * efm * ofm
         g[EXPAND : EXPAND + 64] += scaled[:, :128]
         g[EXPAND + 64 : EXPAND + 128] += scaled[:, 128:]
-        byw = part * ew[...]
+        byw = part * ew[...].astype(F32)
         fac = put(fac, m, jnp.sum(byw * ofm, axis=1, keepdims=True))
-        nf[1, m] = jnp.sum(byw * ef, axis=0, keepdims=True)
+        nf[1, m] = jnp.sum(byw * efm, axis=0, keepdims=True)
         return acc, pack(2, m, edge), fac
 
     acc, edge, fac = lax.fori_loop(0, 4, upstream_of, (zero, zero, zero))
@@ -333,15 +378,15 @@
         acc = sums(m, acc, dpre, dpre * normed)
 
         low = dq[m, 64:128, 128:1152]
-        sf = sfc[m]
+        sfm = cols[8, m]
         byf = jnp.zeros((64, 1), F32)
         halves = []
         for p in range(3):
             part = dot(hq[m, :, p * 128 : p * 128 + 1024], low, 1, 1)
-            byw = jnp.sum(part * sw[p * 192 : p * 192 + 192], axis=1, keepdims=True)
-            byf = byf + byw[0:64] + byw[64:128] + byw[128:192]
             for q in range(3):
-                halves.append(part[q * 64 : q * 64 + 64] * sf)
+                tap = part[q * 64 : q * 64 + 64]
+                byf = byf + jnp.sum(tap * sw[3 * p + q].astype(F32), axis=1, keepdims=True)
+                halves.append(tap * sfm)
         whole = jnp.concatenate(halves, axis=0)
         whole = jnp.concatenate([whole[:288], whole[288:]], axis=1)
 
@@ -367,7 +412,7 @@
         d = (gain1 * rstd * (dpre1[m] - plain - normed * weighted)).astype(BF16)
         dq[m, 0:64, 0:1024] = d
         part = dot(d, x[m], 1, 1)
-        scaled = part * rf[m]
+        scaled = part * rf[pl.ds(m, 1), :]
         g[REDUCE : REDUCE + 64] += scaled[:, :128]
         g[REDUCE + 64 : REDUCE + 128] += scaled[:, 128:]
         nf[0, m] = jnp.sum(part * rwt[...], axis=0, keepdims=True)
@@ -386,17 +431,16 @@
     start()
 
     def grad_of(m, _):
-        def chunk(j, _):
-            o = pl.multiple_of(j * 256, 256)
-            t = dot(w1[m], dq[m, 0:64, pl.ds(o, 256)], 0, 0)
-            c[m, :, pl.ds(o, 256)] = (u[m, :, pl.ds(o, 256)] + t).astype(BF16)
-            return 0
-
-        lax.fori_loop(0, 4, chunk, 0)
+        for j in range(4):
+            o = j * 256
+            t = u[m, :, o : o + 256] + dot(w1[m], dq[m, 0:64, o : o + 256], 0, 0)
+            wide[pl.ds(2 * j, 256, stride=8), :] = t[:, :128]
+            wide[pl.ds(2 * j + 1, 256, stride=8), :] = t[:, 128:]
+        craw[m] = wide[...].reshape(256, 8, 128).astype(BF16)
         return 0
 
     lax.fori_loop(0, 4, grad_of, 0)
-    stores = [pltpu.make_async_copy(c.at[m], out_hbm.at[m], st_sem.at[m]) for m in range(4)]
+    stores = [pltpu.make_async_copy(craw.at[m], y_hbm.at[m], st_sem.at[m]) for m in range(4)]
     for copy in stores:
         copy.start()
 
@@ -411,35 +455,54 @@
     start()
     wait()
 
-    def rows(at_row, n):
-        return jnp.concatenate(
-            [r3[r // CHUNK, r % CHUNK : r % CHUNK + 8] for r in range(at_row, at_row + n, 8)], axis=0
-        )
-
-    e = rows(EXPAND, 128)
-    o_expand[...] = jnp.concatenate([e[:64], e[64:]], axis=1)
-    e = rows(REDUCE, 128)
-    o_reduce[...] = jnp.transpose(jnp.concatenate([e[:64], e[64:]], axis=1))
-    e = rows(SPATIAL, 288)
-    o_spatial[0:288] = e[:, :64]
-    o_spatial[288:576] = e[:, 64:]
-    e = rows(REDUCE_F, 8)
-    o_rf[...] = jnp.concatenate([e[:4], e[4:]], axis=1)
-    e = rows(OUTPUT_F, 8)
-    o_of[...] = jnp.concatenate([e[:4], e[4:]], axis=1)
-    e = rows(COLUMN_F, 8)
-    o_ef[...] = e[:4, :64]
-    o_sf[...] = e[4:, :64]
-    o_norm[...] = jnp.concatenate(
+    for r in range(0, 640, 8):
+        packed[r : r + 8] = r3[r // CHUNK, r % CHUNK : r % CHUNK + 8]
+    packed[NORMS : NORMS + 8] = jnp.concatenate(
         [
             jnp.sum(stats1[4:8], axis=0, keepdims=True),
             jnp.sum(stats1[0:4], axis=0, keepdims=True),
             jnp.sum(stats2[4:8], axis=0, keepdims=True),
             jnp.sum(stats2[0:4], axis=0, keepdims=True),
+            jnp.zeros((4, 128), F32),
         ],
         axis=0,
-    )[:, :64]
+    )
     for copy in stores:
+        copy.wait()
+
+
+def unpack(
+    y_hbm, packed_hbm,
+    out_hbm, o_reduce, o_spatial, o_expand, o_rf, o_sf, o_ef, o_of, o_g1, o_b1, o_g2, o_b2,
+    y, packed, sem,
+):
+    load = [pltpu.make_async_copy(packed_hbm, packed, sem.at[0])]
+    load += [pltpu.make_async_copy(y_hbm.at[m], y.at[m], sem.at[1 + m]) for m in range(4)]
+    store = [pltpu.make_async_copy(y.at[m], out_hbm.at[m], sem.at[5 + m]) for m in range(4)]
+    for copy in load:
+        copy.start()
+    load[0].wait()
+    o_expand[:, :128] = packed[EXPAND : EXPAND + 64]
+    o_expand[:, 128:] = packed[EXPAND + 64 : EXPAND + 128]
+    o_reduce[:, :128] = packed[REDUCE : REDUCE + 64]
+    o_reduce[:, 128:] = packed[REDUCE + 64 : REDUCE + 128]
+    for k in range(9):
+        r = k * 64
+        for t in range(r, r + 64, 32):
+            at_row = SPATIAL + t % 288
+            half = slice(0, 64) if t < 288 else slice(64, 128)
+            o_spatial[k, t - r : t - r + 32] = packed[at_row : at_row + 32, half]
+    for o, at_row in ((o_rf, REDUCE_F), (o_of, OUTPUT_F)):
+        o[:, :128] = packed[at_row : at_row + 4]
+        o[:, 128:] = packed[at_row + 4 : at_row + 8]
+    o_ef[...] = packed[COLUMN_F : COLUMN_F + 4, :64]
+    o_sf[...] = packed[COLUMN_F + 4 : COLUMN_F + 8, :64]
+    for n, o in enumerate((o_g1, o_b1, o_g2, o_b2)):
+        o[...] = packed[NORMS + n : NORMS + n + 1, :64]
+    for m in range(4):
+        load[1 + m].wait()
+        store[m].start()
+    for copy in store:
         copy.wait()
 
 
@@ -448,28 +511,34 @@
     reduce_factor, spatial_factor, expand_factor, output_factor,
     gain_first, shift_first, gain_second, shift_second,
 ):
-    rw = reduce_weight.astype(F32)
-    sw = spatial_weight.astype(F32)
-    ew = expand_weight.astype(F32)
-    rwt = rw.T
-    w1 = (reduce_factor[:, None, :] * rwt[None]).astype(BF16)
-    spatial = (spatial_factor[:, None, :, None] * sw[None]).astype(BF16)
-    w2 = spatial.reshape(4, 3, 192, 64)
-    w2b = spatial.reshape(4, 3, 3, 64, 64)[:, ::-1, ::-1].transpose(0, 1, 3, 2, 4).reshape(4, 3, 64, 192)
-    w3 = (expand_factor[:, :, None] * ew[None] * output_factor[:, None, :]).astype(BF16)
-    gb = jnp.stack([gain_first, shift_first, gain_second, shift_second])[:, :, None]
     vmem = pl.BlockSpec(memory_space=pltpu.VMEM)
     hbm = pl.BlockSpec(memory_space=pl.ANY)
     sds = jax.ShapeDtypeStruct
-    outs = pl.pallas_call(
+    y, packed = pl.pallas_call(
         kernel,
-        out_shape=(
-            sds((4, 256, 1024), BF16), sds((256, 64), F32), sds((576, 64), F32), sds((64, 256), F32),
-            sds((4, 256), F32), sds((4, 64), F32), sds((4, 64), F32), sds((4, 256), F32), sds((4, 64), F32),
-        ),
-        in_specs=[hbm, hbm] + [vmem] * 12,
-        out_specs=(hbm,) + (vmem,) * 8,
+        out_shape=(sds((4, 256, 8, 128), BF16), sds((16 * CHUNK, 128), F32)),
+        in_specs=[hbm] * 13,
+        out_specs=(hbm, vmem),
         scratch_shapes=[
+            pltpu.VMEM((4, 256, 8, 128), BF16),
+            pltpu.VMEM((4, 256, 8, 128), BF16),
+            pltpu.VMEM((2048, 128), F32),
+            pltpu.VMEM((64, 256), BF16),
+            pltpu.VMEM((9, 64, 64), BF16),
+            pltpu.VMEM((64, 256), BF16),
+            pltpu.VMEM((4, 256), F32),
+            pltpu.VMEM((4, 64), F32),
+            pltpu.VMEM((4, 64), F32),
+            pltpu.VMEM((4, 256), F32),
+            pltpu.VMEM((1, 64), F32),
+            pltpu.VMEM((1, 64), F32),
+            pltpu.VMEM((1, 64), F32),
+            pltpu.VMEM((1, 64), F32),
+            pltpu.VMEM((4, 64, 256), BF16),
+            pltpu.VMEM((4, 3, 192, 64), BF16),
+            pltpu.VMEM((4, 3, 64, 192), BF16),
+            pltpu.VMEM((4, 64, 256), BF16),
+            pltpu.VMEM((64, 256), F32),
             pltpu.VMEM((4, 256, 1024), BF16),
             pltpu.VMEM((4, 256, 1024), BF16),
             pltpu.VMEM((4, 256, 1024), F32),
@@ -486,8 +555,8 @@
             pltpu.VMEM((16, CHUNK, 128), F32),
             pltpu.VMEM((16, CHUNK, 128), F32),
             pltpu.VMEM((16, CHUNK, 128), F32),
-            pltpu.VMEM((8, 4, 64, 1), F32),
-            pltpu.SemaphoreType.DMA((8,)),
+            pltpu.VMEM((12, 4, 64, 1), F32),
+            pltpu.SemaphoreType.DMA((20,)),
             pltpu.SemaphoreType.DMA((4,)),
             pltpu.SemaphoreType.DMA((11, 16)),
             pltpu.SemaphoreType.DMA((11, 16)),
@@ -495,18 +564,32 @@
             pltpu.SemaphoreType.DMA((3, 8)),
         ],
         compiler_params=pltpu.CompilerParams(
-            collective_id=0, has_side_effects=True, vmem_limit_bytes=56 * 1024 * 1024
+            collective_id=0, has_side_effects=True, vmem_limit_bytes=67043328
         ),
+        name="step",
     )(
-        features.reshape(4, 256, 1024), cotangent.reshape(4, 256, 1024), w1, w2, w2b, w3,
-        rwt, sw.reshape(576, 64), ew, reduce_factor[:, None, :], output_factor[:, None, :],
-        spatial_factor[:, :, None], expand_factor[:, :, None], gb,
+        features, cotangent, reduce_weight.T, spatial_weight, expand_weight,
+        reduce_factor, spatial_factor, expand_factor, output_factor,
+        gain_first.reshape(1, 64), shift_first.reshape(1, 64),
+        gain_second.reshape(1, 64), shift_second.reshape(1, 64),
     )
-    grad, o_reduce, o_spatial, o_expand, o_rf, o_sf, o_ef, o_of, o_norm = outs
-    return (
-        grad.reshape(4, 256, 8, 128), o_reduce, o_spatial.reshape(9, 64, 64), o_expand,
-        o_rf, o_sf, o_ef, o_of, o_norm[0], o_norm[1], o_norm[2], o_norm[3],
-    )
+    outs = pl.pallas_call(
+        unpack,
+        out_shape=(
+            sds((4, 256, 8, 128), BF16), sds((64, 256), F32), sds((9, 64, 64), F32), sds((64, 256), F32),
+            sds((4, 256), F32), sds((4, 64), F32), sds((4, 64), F32), sds((4, 256), F32),
+        ) + (sds((1, 64), F32),) * 4,
+        in_specs=[hbm, hbm],
+        out_specs=(hbm,) + (vmem,) * 11,
+        scratch_shapes=[
+            pltpu.VMEM((4, 256, 8, 128), BF16),
+            pltpu.VMEM((16 * CHUNK, 128), F32),
+            pltpu.SemaphoreType.DMA((9,)),
+        ],
+        compiler_params=pltpu.CompilerParams(vmem_limit_bytes=67043328),
+        name="unpack",
+    )(y, packed)
+    return (outs[0], outs[1].T) + outs[2:8] + tuple(o.reshape(64) for o in outs[8:])
 
 
 def solution(mesh):

time: 133 us -> 105 us (0.79)
  local copies, waits for them, and re-layouts: 23.4 us -> 0 us
  other arithmetic: 5.97 us -> 0 us
  Pallas kernels: 102 us -> 104 us
    unnamed x34 -> x0, local copies, waits for them, and re-layouts: 8.06 us -> none
    reshape x3 -> x0, local copies, waits for them, and re-layouts: 7.61 us -> none  [the longest x1 4.3 us: body(): features.reshape(4, 256, 1024)]
    broadcast_in_dim x5 -> x0, local copies, waits for them, and re-layouts: 6.22 us -> none  [the longest x1 1.45 us: body(): expand_factor[:, :, None] * ew[None] * output_factor[:, None, :]]
    convert_element_type x5 -> x0, other arithmetic: 4.49 us -> none  [the longest x1 1.47 us: body(): (expand_factor[:, :, None] * ew[None] * output_factor[:, None, :]).astype...]
    pallas_call x1 -> x2, Pallas kernels: 102 us -> 104 us  [the longest x1 101 us: body(): pl.pallas_call(kernel, out_shape=(sds((4, 256, 8, 128), BF16), sds((16 *...]
where the time goes in v2:
time: 105 us
  Pallas kernels  104 us (99%)
    pallas_call x1, Pallas kernels, body(): pl.pallas_call(kernel, out_shape=(sds((4, 256, 8, 128), BF16), sds((16 *...  101 us
    pallas_call x1, Pallas kernels, body(): pl.pallas_call(unpack, out_shape=(sds((4, 256, 8, 128), BF16), sds((64, 2...  3.31 us

profile of v2, /device:TPU:1, one launch (start us, length us, event | category | flops | bytes accessed | tf_op | source)
XLA Modules:
  0.0 104.9 jit_solution(4507228077050098097)
XLA Ops:
  0.6 101.0 %step.1 = (bf16[4,256,8,128]{3,2,1,0:T(8,128)(2,1)}, f32[640,128]{1,0:T(8,128)}) custom-call(bf16[4,256,8,128]{3,2,1,0:T(8,128)(2,1)} %x_hbm.1, bf16[4,256,8,128]{3,2,1,0:T(8,128)(2,1)} %c_hbm.1, bf16[64,256]{1,0:T(8,128)(2,1)} %bitcast.10, bf16[9,64,64]{2,1,0:T(8,128)(2,1)} %sw_hbm.1, bf16[64,256]{1,0:T(8,128)(2,1)} %ew_hbm.1, f32[4,256]{1,0:T(4,128)} %rf_hbm.1, ...), custom_call_target="tpu_custom_call" | custom-call | tf_op jit(solution)/shard_map/step/pallas_call | solution.py:517
  101.6 3.3 %unpack.1 = (bf16[4,256,8,128]{3,2,1,0:T(8,128)(2,1)}, f32[64,256]{1,0:T(8,128)}, f32[9,64,64]{2,1,0:T(8,128)}, f32[64,256]{1,0:T(8,128)}, f32[4,256]{1,0:T(4,12...) custom-call(bf16[4,256,8,128]{3,2,1,0:T(8,128)(2,1)} %get-tuple-elem, ...), custom_call_target="tpu_custom_call" | custom-call | tf_op jit(solution)/shard_map/unpack/pallas_call | solution.py:576

commit v3 on v2

v3 whole, which is shorter than its diff:
```python
import functools

import jax
import jax.numpy as jnp
from jax import lax
from jax.experimental import pallas as pl
from jax.experimental.pallas import tpu as pltpu
from jax.sharding import Mesh
from jax.sharding import PartitionSpec as P

ROWS = ("rows_0", "rows_1")
COLS = ("cols_0", "cols_1", "cols_2")
MESH = pl.DeviceIdType.MESH
EPSILON = 1e-05
F32 = jnp.float32
BF16 = jnp.bfloat16

SHARE, WITH_PART = 40, 48
REDUCE_F, OUTPUT_F, COLUMN_F, TILES = 36, 37, 38, 48
NORMS = 16 * WITH_PART


def other(t):
    return t % 16, 16 + 8 * (t // 16)


def dot(a, b, ca, cb):
    return lax.dot_general(a, b, (((ca,), (cb,)), ((), ())), preferred_element_type=F32)


def sigmoid(v):
    return 0.5 + 0.5 * jnp.tanh(0.5 * v)


def silu(v):
    return v * sigmoid(v)


def slope(v):
    s = sigmoid(v)
    return s * (1.0 + v * (1.0 - s))


def total(buf):
    t = buf[0]
    for k in range(1, 16):
        t = t + buf[k]
    return t


def kernel(
    x_hbm, c_hbm, rw_hbm, sw_hbm, ew_hbm, rf_hbm, sf_hbm, ef_hbm, of_hbm, g1_hbm, b1_hbm, g2_hbm, b2_hbm,
    y_hbm, packed,
    xraw, craw, wide, rw, sw, ew, rf, sf, ef, of, g1, b1, g2, b2,
    w1, w2, w2b, w3, rwt,
    x, c, u, ulow, h2, hb, hq, dq, dpre1, nf, pk, pr, arb, ara,
    acce, accr, accs, sxs, bn, bn1, bn2, bnc, g, r1, r2, r3, cols,
    ld_sem, st_sem, s_sem, r_sem, hs_sem, hr_sem,
):
    count = float(64 * 4096)
    x_hi, y = lax.axis_index("rows_0"), lax.axis_index("rows_1")
    z, x_lo, core = lax.axis_index("cols_0"), lax.axis_index("cols_1"), lax.axis_index("cols_2")
    row = x_hi * 4 + y
    col = z * 4 + x_lo * 2 + core
    rank_a = x_hi * 8 + x_lo * 4 + y
    rank_b = z * 2 + core

    def peer_a(d):
        a = lax.rem(rank_a + d, 16)
        return (lax.div(a, 8), lax.rem(a, 4), z, lax.rem(lax.div(a, 4), 2), core)

    def peer_b(d):
        b = lax.rem(rank_b + d, 16)
        return (x_hi, y, lax.div(b, 2), x_lo, lax.rem(b, 2))

    def at(dr, dc):
        rr, cc = lax.rem(row + dr + 8, 8), lax.rem(col + dc + 32, 32)
        return (lax.div(rr, 4), lax.rem(rr, 4), lax.div(cc, 4), lax.rem(lax.div(cc, 2), 2), lax.rem(cc, 2))

    sides = ((0, 1), (0, -1), (1, 1), (1, -1), (-1, 1), (-1, -1))

    pairs = (
        (rw_hbm, rw), (rf_hbm, rf), (sw_hbm, sw), (ew_hbm, ew), (sf_hbm, sf), (ef_hbm, ef), (of_hbm, of),
        (g1_hbm, g1), (b1_hbm, b1), (g2_hbm, g2), (b2_hbm, b2),
    )
    load_w = [pltpu.make_async_copy(a, b, ld_sem.at[8 + n]) for n, (a, b) in enumerate(pairs)]
    load_x = [pltpu.make_async_copy(x_hbm.at[m], xraw.at[m], ld_sem.at[m]) for m in range(4)]
    load_c = [pltpu.make_async_copy(c_hbm.at[m], craw.at[m], ld_sem.at[4 + m]) for m in range(4)]
    for copy in load_w[:2] + load_x + load_w[2:] + load_c:
        copy.start()

    barrier = pltpu.get_barrier_semaphore()

    def greet(d, _):
        pl.semaphore_signal(barrier, inc=1, device_id=peer_a(d), device_id_type=MESH)
        pl.semaphore_signal(barrier, inc=1, device_id=peer_b(d), device_id_type=MESH)
        return 0

    lax.fori_loop(1, 16, greet, 0)
    for side in sides:
        pl.semaphore_signal(barrier, inc=1, device_id=at(*side), device_id_type=MESH)

    def exchange(stage, src, buf, rank, peer):
        def copy(d):
            return pltpu.make_async_remote_copy(
                src_ref=src(d), dst_ref=buf.at[rank], send_sem=s_sem.at[stage, d],
                recv_sem=r_sem.at[stage, d], device_id=peer(d), device_id_type=MESH,
            )

        def start(d, _):
            copy(d).start()
            return 0

        def wait(d, _):
            copy(d).wait()
            return 0

        lax.fori_loop(1, 16, start, 0)
        return lambda: lax.fori_loop(1, 16, wait, 0)

    def sum_start(k, n, tile):
        arb[2 * k + n, rank_b] = tile
        return exchange(
            4 * k + 2 * n, lambda d: arb.at[2 * k + n, rank_b], arb.at[2 * k + n], rank_b, peer_b
        )

    def sum_middle(k, n, wait):
        wait()
        ara[2 * k + n, rank_a] = total(arb.at[2 * k + n])
        return exchange(
            4 * k + 2 * n + 1, lambda d: ara.at[2 * k + n, rank_a], ara.at[2 * k + n], rank_a, peer_a
        )

    def sum_end(k, n, wait):
        wait()
        return total(ara.at[2 * k + n])

    def halo(k, n):
        members = pl.ds(2 * n, 2)
        copies = [
            pltpu.make_async_remote_copy(
                src_ref=hb.at[k, members, :, pl.ds(128, 128)],
                dst_ref=hb.at[k, members, :, pl.ds(1152, 128)],
                send_sem=hs_sem.at[2 * k + n, 6], recv_sem=hr_sem.at[2 * k + n, 6],
                device_id=at(-1, 0), device_id_type=MESH,
            ),
            pltpu.make_async_remote_copy(
                src_ref=hb.at[k, members, :, pl.ds(1024, 128)],
                dst_ref=hb.at[k, members, :, pl.ds(0, 128)],
                send_sem=hs_sem.at[2 * k + n, 7], recv_sem=hr_sem.at[2 * k + n, 7],
                device_id=at(1, 0), device_id_type=MESH,
            ),
        ]
        for e, side in enumerate(sides):
            copies.append(
                pltpu.make_async_remote_copy(
                    src_ref=pk.at[k, n], dst_ref=pr.at[k, n, e], send_sem=hs_sem.at[2 * k + n, e],
                    recv_sem=hr_sem.at[2 * k + n, e], device_id=at(*side), device_id_type=MESH,
                )
            )
        for copy in copies:
            copy.start()
        return copies

    lane = lax.broadcasted_iota(jnp.int32, (64, 128), 1)
    sub = lax.broadcasted_iota(jnp.int32, (8, 128), 0)
    zero = jnp.zeros((64, 128), F32)

    def put(acc, n, value):
        return jnp.where(lane == n, value, acc)

    def rows_of_columns(acc):
        return jnp.transpose(jnp.concatenate([acc, jnp.zeros((64, 128), F32)], axis=0))[:8]

    def columns_of_rows(tile, k, members):
        t = jnp.transpose(jnp.concatenate([tile, jnp.zeros((120, 128), F32)], axis=0))
        for m in members:
            cols[k, m] = t[:64, m : m + 1]
            cols[k + 1, m] = t[:64, 4 + m : 5 + m]

    def sums(m, acc, a, b):
        acc = put(acc, m, jnp.sum(a, axis=1, keepdims=True))
        return put(acc, 4 + m, jnp.sum(b, axis=1, keepdims=True))

    def pack(k, n):
        acc = zero
        for m in group(n):
            for i in range(8):
                t = hb[k, m, :, 128 + i * 128 : 256 + i * 128]
                acc = put(acc, m * 8 + i, t[:, 0:1])
                acc = put(acc, 32 + m * 8 + i, t[:, 127:128])
        pk[k, n] = acc

    def group(n):
        return (2 * n, 2 * n + 1)

    top = jnp.where(row > 0, 1.0, 0.0).astype(F32)
    bottom = jnp.where(row < 7, 1.0, 0.0).astype(F32)
    left = jnp.where(col > 0, 1.0, 0.0).astype(F32)
    right = jnp.where(col < 31, 1.0, 0.0).astype(F32)
    masks = (left, right, top * left, top * right, bottom * left, bottom * right)

    def spread(dst, m, tile, edge):
        edges = [edge(e) * masks[e] for e in range(6)]
        for i in range(10):
            t = tile(i)
            if i == 0:
                t, e0, e2, at_row = t * top, edges[2], edges[3], 7
            elif i == 9:
                t, e0, e2, at_row = t * bottom, edges[4], edges[5], 0
            else:
                e0, e2, at_row = edges[0], edges[1], i - 1
            where0 = 32 + m * 8 + at_row
            where2 = m * 8 + at_row
            before = jnp.where(
                lane == 0, pltpu.roll(e0, 128 - where0, axis=1), pltpu.roll(t, 1, axis=1)
            )
            after = jnp.where(
                lane == 127, pltpu.roll(e2, 127 - where2, axis=1), pltpu.roll(t, 127, axis=1)
            )
            span = slice(i * 128, i * 128 + 128)
            dst[m, 0:64, span] = before.astype(BF16)
            dst[m, 64:128, span] = t.astype(BF16)
            dst[m, 128:192, span] = after.astype(BF16)

    def flatten(src, dst, m):
        wide[m % 2] = src[m].astype(F32).reshape(2048, 128)
        for i in range(8):
            dst[m, :, i * 128 : i * 128 + 128] = wide[m % 2, pl.ds(i, 256, stride=8), :].astype(BF16)

    def moments(k, tile, members):
        columns_of_rows(tile, k, members)
        for m in members:
            mean = cols[k, m] / count
            var = cols[k + 1, m] / count - mean * mean
            cols[k, m] = mean
            cols[k + 1, m] = lax.rsqrt(var + EPSILON)

    for copy in load_w[:2]:
        copy.wait()
    rwt[...] = rw[...].astype(F32)
    for m in range(4):
        w1[m] = (rwt[...] * rf[m : m + 1]).astype(BF16)
    ones = jnp.ones((8, 1024), BF16)

    def free_rows(m):
        base = 2 if m < 2 else 0
        return (base + 4 * (m % 2), base + 4 * (m % 2) + 1)

    stats, halos = [None, None], [None, None]
    for n in range(2):
        acc = zero
        extra = []
        for m in group(n):
            load_x[m].wait()
            flatten(xraw, x, m)
            a = dot(w1[m], x[m], 1, 0)
            hb[0, m, :, 128:1152] = a
            acc = sums(m, acc, a, a * a)
            extra.append((m, dot(ones, x[m], 1, 1)))
        pack(0, n)
        tile = rows_of_columns(acc)
        for m, e in extra:
            for h, r in enumerate(free_rows(m)):
                tile = jnp.where(sub == r, e[:, h * 128 : h * 128 + 128], tile)
        if n == 0:
            pl.semaphore_wait(barrier, 36)
        stats[n] = sum_start(0, n, tile)
        halos[n] = halo(0, n)

    for copy in load_w[2:]:
        copy.wait()
    tail = jnp.zeros((8, 64), F32)
    columns_of_rows(
        jnp.concatenate([jnp.concatenate([sf[...], ef[...]], axis=0), tail], axis=1), 8, range(4)
    )
    columns_of_rows(
        jnp.concatenate(
            [jnp.concatenate([g1[...], b1[...], g2[...], b2[...], tail[:4]], axis=0), tail], axis=1
        ), 10, range(4),
    )
    for m in range(4):
        sfm, efm = cols[8, m], cols[9, m]
        w3[m] = (efm * ew[...].astype(F32) * of[m : m + 1]).astype(BF16)
        for p in range(3):
            taps = [(sfm * sw[3 * p + q].astype(F32)).astype(BF16) for q in range(3)]
            for q in range(3):
                w2[m, p, q * 64 : q * 64 + 64] = taps[q]
            w2b[m, 2 - p] = jnp.concatenate(taps[::-1], axis=1)
    gain1, shift1, gain2, shift2 = (cols[10, n] for n in range(4))
    for copy in load_c:
        copy.wait()
    for m in range(2):
        flatten(craw, c, m)
    stats[0] = sum_middle(0, 0, stats[0])
    for m in range(2, 4):
        flatten(craw, c, m)
    stats[1] = sum_middle(0, 1, stats[1])

    for n in range(2):
        tile = sum_end(0, n, stats[n])
        moments(0, tile, group(n))
        for m in group(n):
            for h, r in enumerate(free_rows(m)):
                sxs[m, h] = jnp.broadcast_to(tile[r : r + 1], (8, 128))
        for copy in halos[n]:
            copy.wait()
        acc = zero
        for m in group(n):
            mean, rstd = cols[0, m], cols[1, m]

            def hidden(v):
                return silu(gain1 * ((v - mean) * rstd) + shift1)

            spread(
                hq, m, lambda i: hidden(hb[0, m, :, i * 128 : i * 128 + 128]),
                lambda e: hidden(pr[0, n, e]),
            )
            a = dot(w2[m, 0], hq[m, :, 0:1024], 0, 0)
            a = a + dot(w2[m, 1], hq[m, :, 128:1152], 0, 0)
            a = a + dot(w2[m, 2], hq[m, :, 256:1280], 0, 0)
            hb[1, m, :, 128:1152] = a
            acc = sums(m, acc, a, a * a)
        pack(1, n)
        stats[n] = sum_start(1, n, rows_of_columns(acc))
        halos[n] = halo(1, n)

    def project(m):
        normed = ((hb[0, m, :, 128:1152] - cols[0, m]) * cols[1, m]).astype(BF16)
        part = dot(normed, x[m], 1, 1)
        for a in range(16):
            h, f = a // 8, a % 8
            bn[a, m * 8 : m * 8 + 8] = part[f * 8 : f * 8 + 8, h * 128 : h * 128 + 128]

    project(0)
    project(1)
    stats[0] = sum_middle(1, 0, stats[0])
    project(2)
    project(3)
    stats[1] = sum_middle(1, 1, stats[1])
    features = exchange(16, lambda d: bn.at[lax.rem(rank_a + d, 16)], bn1, rank_a, peer_a)

    sums2 = []
    for n in range(2):
        moments(2, sum_end(1, n, stats[n]), group(n))
        for copy in halos[n]:
            copy.wait()
        acc = zero
        for m in group(n):
            mean, rstd = cols[2, m], cols[3, m]
            for o in range(0, 1024, 256):
                span = slice(o, o + 256)
                pre = gain2 * ((hb[1, m, :, o + 128 : o + 384] - mean) * rstd) + shift2
                s = sigmoid(pre)
                h2[m, :, span] = (pre * s).astype(BF16)
                dpre1[m, :, span] = s * (1.0 + pre * (1.0 - s))
                third = dot(w3[m], h2[m, :, span], 0, 0)
                up = c[m, :, span].astype(F32) * slope(x[m, :, span].astype(F32) + third)
                u[m, :, span] = up
                ulow[m, :, span] = up.astype(BF16)
            back = dot(w3[m], ulow[m], 1, 0)
            hb[2, m, :, 128:1152] = back
            dpre = back * dpre1[m]
            acc = sums(m, acc, dpre, dpre * ((hb[1, m, :, 128:1152] - mean) * rstd))
        pack(2, n)
        stats[n] = sum_start(2, n, rows_of_columns(acc))
        halos[n] = halo(2, n)

    fac = zero

    def expand(m, fac):
        part = dot(h2[m], ulow[m], 1, 1)
        ofm, efm = of[m : m + 1], cols[9, m]
        scaled = part * efm * ofm
        acce[...] = scaled if m == 0 else acce[...] + scaled
        byw = part * ew[...].astype(F32)
        nf[1, m] = jnp.sum(byw * efm, axis=0, keepdims=True)
        return put(fac, m, jnp.sum(byw * ofm, axis=1, keepdims=True))

    fac = expand(1, expand(0, fac))
    stats[0] = sum_middle(2, 0, stats[0])
    fac = expand(3, expand(2, fac))
    stats[1] = sum_middle(2, 1, stats[1])
    features()
    bn1[rank_a] = bn[rank_a]
    bn2[rank_b] = total(bn1)
    features = exchange(17, lambda d: bn2.at[rank_b], bn2, rank_b, peer_b)

    for n in range(2):
        tile = sum_end(2, n, stats[n])
        sums2.append(tile)
        columns_of_rows(tile, 4, group(n))
        for copy in halos[n]:
            copy.wait()
        acc = zero
        for m in group(n):
            mean, rstd, plain, weighted = cols[2, m], cols[3, m], cols[4, m] / count, cols[5, m] / count

            def dact(second, back):
                normed = (second - mean) * rstd
                dpre = back * slope(gain2 * normed + shift2)
                return gain2 * rstd * (dpre - plain - normed * weighted)

            spread(
                dq, m,
                lambda i: dact(hb[1, m, :, i * 128 : i * 128 + 128], hb[2, m, :, i * 128 : i * 128 + 128]),
                lambda e: dact(pr[1, n, e], pr[2, n, e]),
            )
            a = dot(w2b[m, 0], dq[m, :, 0:1024], 1, 0)
            a = a + dot(w2b[m, 1], dq[m, :, 128:1152], 1, 0)
            a = a + dot(w2b[m, 2], dq[m, :, 256:1280], 1, 0)
            normed = (hb[0, m, :, 128:1152] - cols[0, m]) * cols[1, m]
            dpre = a * slope(gain1 * normed + shift1)
            dpre1[m] = dpre
            acc = sums(m, acc, dpre, dpre * normed)
        stats[n] = sum_start(3, n, rows_of_columns(acc))

    def gradients(m, fac):
        sfm = cols[8, m]
        byf = jnp.zeros((64, 1), F32)
        for p in range(3):
            part = dot(hq[m, :, p * 128 : p * 128 + 1024], dq[m, 64:128, 128:1152], 1, 1)
            for q in range(3):
                k = 3 * p + q
                tap = part[q * 64 : q * 64 + 64]
                byf = byf + jnp.sum(tap * sw[k].astype(F32), axis=1, keepdims=True)
                tap = tap * sfm
                accs[k] = tap if m == 0 else accs[k] + tap
        part = dot(dpre1[m].astype(BF16), x[m], 1, 1) * (gain1 * cols[1, m])
        scaled = part * rf[m : m + 1]
        accr[...] = scaled if m == 0 else accr[...] + scaled
        nf[0, m] = jnp.sum(part * rwt[...], axis=0, keepdims=True)
        return put(fac, 4 + m, byf)

    fac = gradients(1, gradients(0, fac))
    stats[0] = sum_middle(3, 0, stats[0])
    fac = gradients(3, gradients(2, fac))
    stats[1] = sum_middle(3, 1, stats[1])
    for a in range(16):
        h, f = a // 8, a % 8
        g[a, 0:8] = acce[f * 8 : f * 8 + 8, h * 128 : h * 128 + 128]
        g[a, 8:16] = accr[f * 8 : f * 8 + 8, h * 128 : h * 128 + 128]
    for t in range(36):
        low, high = t * 8, 288 + t * 8
        a, r = other(t)
        g[a, r : r + 8] = jnp.concatenate(
            [accs[low // 64, low % 64 : low % 64 + 8], accs[high // 64, high % 64 : high % 64 + 8]], axis=1
        )
    for k, t in ((0, REDUCE_F), (1, OUTPUT_F)):
        a, r = other(t)
        g[a, r : r + 8] = jnp.concatenate(
            [nf[k, m, :, h * 128 : h * 128 + 128] for h in range(2) for m in range(4)], axis=0
        )
    a, r = other(COLUMN_F)
    g[a, r : r + 8] = rows_of_columns(fac)
    for t in range(COLUMN_F + 1, TILES):
        a, r = other(t)
        g[a, r : r + 8] = jnp.zeros((8, 128), F32)
    shares = exchange(18, lambda d: g.at[lax.rem(rank_a + d, 16)], r1, rank_a, peer_a)
    features()
    bnc[...] = total(bn2)

    def finish(m):
        mean, rstd, plain, weighted = cols[0, m], cols[1, m], cols[6, m] / count, cols[7, m] / count
        normed = (hb[0, m, :, 128:1152] - mean) * rstd
        dq[m, 0:64, 0:1024] = (gain1 * rstd * (dpre1[m] - plain - normed * weighted)).astype(BF16)
        for j in range(4):
            o = j * 256
            t = u[m, :, o : o + 256] + dot(w1[m], dq[m, 0:64, o : o + 256], 0, 0)
            wide[m % 2, pl.ds(2 * j, 256, stride=8), :] = t[:, :128]
            wide[m % 2, pl.ds(2 * j + 1, 256, stride=8), :] = t[:, 128:]
        craw[m] = wide[m % 2].reshape(256, 8, 128).astype(BF16)
        store = pltpu.make_async_copy(craw.at[m], y_hbm.at[m], st_sem.at[m])
        store.start()
        return store

    tile = sum_end(3, 0, stats[0])
    sums1 = [tile]
    columns_of_rows(tile, 6, group(0))
    stores = [finish(0), finish(1)]
    shares()
    r1[rank_a] = g[rank_a]
    r2[rank_b] = total(r1)
    shares = exchange(19, lambda d: r2.at[rank_b], r2, rank_b, peer_b)
    tile = sum_end(3, 1, stats[1])
    sums1.append(tile)
    columns_of_rows(tile, 6, group(1))
    stores += [finish(2), finish(3)]

    half, block = lax.div(rank_a, 8), pl.ds(pl.multiple_of(lax.rem(rank_a, 8) * 8, 8), 8)
    span = pl.ds(pl.multiple_of(half * 128, 128), 128)
    fix = jnp.zeros((8, 128), F32)
    part = jnp.zeros((8, 128), F32)
    for m in range(4):
        plain, weighted = cols[6, m, block] / count, cols[7, m, block] / count
        e = cols[10, 0, block] * cols[1, m, block] * (
            plain * sxs[m, half] + weighted * bnc[m * 8 : m * 8 + 8]
        )
        fix = fix + e * rf[m : m + 1, span]
        part = jnp.where(
            sub == half * 4 + m, jnp.sum(e * rwt[block, span], axis=0, keepdims=True), part
        )
    shares()
    share = total(r2)
    r3[rank_a, 0:8] = share[0:8]
    r3[rank_a, 8:16] = share[8:16] - fix
    r3[rank_a, 16:40] = share[16:40]
    r3[rank_a, 40:48] = part
    shares = exchange(20, lambda d: r3.at[rank_a], r3, rank_a, peer_a)
    first, second = sums1[0] + sums1[1], sums2[0] + sums2[1]
    packed[NORMS : NORMS + 8] = jnp.concatenate(
        [
            jnp.sum(first[4:8], axis=0, keepdims=True),
            jnp.sum(first[0:4], axis=0, keepdims=True),
            jnp.sum(second[4:8], axis=0, keepdims=True),
            jnp.sum(second[0:4], axis=0, keepdims=True),
            jnp.zeros((4, 128), F32),
        ],
        axis=0,
    )
    shares()
    for a in range(16):
        packed[a * WITH_PART : a * WITH_PART + WITH_PART] = r3[a]
    for copy in stores:
        copy.wait()


def unpack(
    y_hbm, packed_hbm,
    out_hbm, o_reduce, o_spatial, o_expand, o_rf, o_sf, o_ef, o_of, o_g1, o_b1, o_g2, o_b2,
    y, packed, sem,
):
    load = [pltpu.make_async_copy(packed_hbm, packed, sem.at[0])]
    load += [pltpu.make_async_copy(y_hbm.at[m], y.at[m], sem.at[1 + m]) for m in range(4)]
    store = [pltpu.make_async_copy(y.at[m], out_hbm.at[m], sem.at[5 + m]) for m in range(4)]
    for copy in load:
        copy.start()
    for m in range(4):
        load[1 + m].wait()
        store[m].start()
    load[0].wait()

    def tile(a, r):
        return packed[a * WITH_PART + r : a * WITH_PART + r + 8]

    fix = jnp.zeros((8, 128), F32)
    for a in range(16):
        h, f = a // 8, a % 8
        o_expand[f * 8 : f * 8 + 8, h * 128 : h * 128 + 128] = tile(a, 0)
        o_reduce[f * 8 : f * 8 + 8, h * 128 : h * 128 + 128] = tile(a, 8)
        fix = fix + tile(a, 40)
    for t in range(36):
        both = tile(*other(t))
        for n in range(2):
            r = n * 288 + t * 8
            o_spatial[r // 64, r % 64 : r % 64 + 8] = both[:, n * 64 : n * 64 + 64]
    for o, e in ((o_rf, tile(*other(REDUCE_F)) - fix), (o_of, tile(*other(OUTPUT_F)))):
        o[:, :128] = e[:4]
        o[:, 128:] = e[4:]
    e = tile(*other(COLUMN_F))
    o_ef[...] = e[:4, :64]
    o_sf[...] = e[4:, :64]
    for n, o in enumerate((o_g1, o_b1, o_g2, o_b2)):
        o[...] = packed[NORMS + n : NORMS + n + 1, :64]
    for copy in store:
        copy.wait()


def body(
    features, cotangent, reduce_weight, spatial_weight, expand_weight,
    reduce_factor, spatial_factor, expand_factor, output_factor,
    gain_first, shift_first, gain_second, shift_second,
):
    vmem = pl.BlockSpec(memory_space=pltpu.VMEM)
    hbm = pl.BlockSpec(memory_space=pl.ANY)
    sds = jax.ShapeDtypeStruct
    y, packed = pl.pallas_call(
        kernel,
        out_shape=(sds((4, 256, 8, 128), BF16), sds((NORMS + 8, 128), F32)),
        in_specs=[hbm] * 13,
        out_specs=(hbm, vmem),
        scratch_shapes=[
            pltpu.VMEM((4, 256, 8, 128), BF16),
            pltpu.VMEM((4, 256, 8, 128), BF16),
            pltpu.VMEM((2, 2048, 128), F32),
            pltpu.VMEM((64, 256), BF16),
            pltpu.VMEM((9, 64, 64), BF16),
            pltpu.VMEM((64, 256), BF16),
            pltpu.VMEM((4, 256), F32),
            pltpu.VMEM((4, 64), F32),
            pltpu.VMEM((4, 64), F32),
            pltpu.VMEM((4, 256), F32),
            pltpu.VMEM((1, 64), F32),
            pltpu.VMEM((1, 64), F32),
            pltpu.VMEM((1, 64), F32),
            pltpu.VMEM((1, 64), F32),
            pltpu.VMEM((4, 64, 256), BF16),
            pltpu.VMEM((4, 3, 192, 64), BF16),
            pltpu.VMEM((4, 3, 64, 192), BF16),
            pltpu.VMEM((4, 64, 256), BF16),
            pltpu.VMEM((64, 256), F32),
            pltpu.VMEM((4, 256, 1024), BF16),
            pltpu.VMEM((4, 256, 1024), BF16),
            pltpu.VMEM((4, 256, 1024), F32),
            pltpu.VMEM((4, 256, 1024), BF16),
            pltpu.VMEM((4, 64, 1024), BF16),
            pltpu.VMEM((3, 4, 64, 1280), F32),
            pltpu.VMEM((4, 192, 1280), BF16),
            pltpu.VMEM((4, 192, 1280), BF16),
            pltpu.VMEM((4, 64, 1024), F32),
            pltpu.VMEM((2, 4, 1, 256), F32),
            pltpu.VMEM((3, 2, 64, 128), F32),
            pltpu.VMEM((3, 2, 6, 64, 128), F32),
            pltpu.VMEM((8, 16, 8, 128), F32),
            pltpu.VMEM((8, 16, 8, 128), F32),
            pltpu.VMEM((64, 256), F32),
            pltpu.VMEM((64, 256), F32),
            pltpu.VMEM((9, 64, 64), F32),
            pltpu.VMEM((4, 2, 8, 128), F32),
            pltpu.VMEM((16, 32, 128), F32),
            pltpu.VMEM((16, 32, 128), F32),
            pltpu.VMEM((16, 32, 128), F32),
            pltpu.VMEM((32, 128), F32),
            pltpu.VMEM((16, SHARE, 128), F32),
            pltpu.VMEM((16, SHARE, 128), F32),
            pltpu.VMEM((16, SHARE, 128), F32),
            pltpu.VMEM((16, WITH_PART, 128), F32),
            pltpu.VMEM((12, 4, 64, 1), F32),
            pltpu.SemaphoreType.DMA((20,)),
            pltpu.SemaphoreType.DMA((4,)),
            pltpu.SemaphoreType.DMA((21, 16)),
            pltpu.SemaphoreType.DMA((21, 16)),
            pltpu.SemaphoreType.DMA((6, 8)),
            pltpu.SemaphoreType.DMA((6, 8)),
        ],
        compiler_params=pltpu.CompilerParams(
            collective_id=0, has_side_effects=True, vmem_limit_bytes=67043328
        ),
        name="step",
    )(
        features, cotangent, reduce_weight.T, spatial_weight, expand_weight,
        reduce_factor, spatial_factor, expand_factor, output_factor,
        gain_first.reshape(1, 64), shift_first.reshape(1, 64),
        gain_second.reshape(1, 64), shift_second.reshape(1, 64),
    )
    outs = pl.pallas_call(
        unpack,
        out_shape=(
            sds((4, 256, 8, 128), BF16), sds((64, 256), F32), sds((9, 64, 64), F32), sds((64, 256), F32),
            sds((4, 256), F32), sds((4, 64), F32), sds((4, 64), F32), sds((4, 256), F32),
        ) + (sds((1, 64), F32),) * 4,
        in_specs=[hbm, hbm],
        out_specs=(hbm,) + (vmem,) * 11,
        scratch_shapes=[
            pltpu.VMEM((4, 256, 8, 128), BF16),
            pltpu.VMEM((NORMS + 8, 128), F32),
            pltpu.SemaphoreType.DMA((9,)),
        ],
        compiler_params=pltpu.CompilerParams(vmem_limit_bytes=67043328),
        name="unpack",
    )(y, packed)
    return (outs[0], outs[1].T) + outs[2:8] + tuple(o.reshape(64) for o in outs[8:])


def solution(mesh):
    split = Mesh(
        mesh.devices.reshape(2, 4, 8, 2, 2), ("rows_0", "rows_1", "cols_0", "cols_1", "cols_2")
    )
    image = P(None, None, ROWS, COLS)
    return jax.shard_map(
        body,
        mesh=split,
        in_specs=(image, image) + (P(),) * 11,
        out_specs=(image,) + (P(),) * 11,
        check_vma=False,
    )
```

time: 105 us -> 96.9 us (0.923)
  Pallas kernels: 104 us -> 95.9 us
    pallas_call x1, Pallas kernels: 101 us -> 92.6 us  [body(): pl.pallas_call(kernel, out_shape=(sds((4, 256, 8, 128), BF16), sds((NORMS...]
where the time goes in v3:
time: 96.9 us; the launch traced here: 96.7 us
  Pallas kernels  95.9 us (99%)
    pallas_call x1, Pallas kernels, body(): pl.pallas_call(kernel, out_shape=(sds((4, 256, 8, 128), BF16), sds((NORMS...  92.6 us
    pallas_call x1, Pallas kernels, body(): pl.pallas_call(unpack, out_shape=(sds((4, 256, 8, 128), BF16), sds((64, 2...  3.33 us

profile of v3, /device:TPU:1, one launch (start us, length us, event | category | flops | bytes accessed | tf_op | source)
XLA Modules:
  0.0 96.7 jit_solution(12905785868327154246)
XLA Ops:
  0.6 92.6 %step.1 = (bf16[4,256,8,128]{3,2,1,0:T(8,128)(2,1)}, f32[776,128]{1,0:T(8,128)}) custom-call(bf16[4,256,8,128]{3,2,1,0:T(8,128)(2,1)} %x_hbm.1, bf16[4,256,8,128]{3,2,1,0:T(8,128)(2,1)} %c_hbm.1, bf16[64,256]{1,0:T(8,128)(2,1)} %bitcast.10, bf16[9,64,64]{2,1,0:T(8,128)(2,1)} %sw_hbm.1, bf16[64,256]{1,0:T(8,128)(2,1)} %ew_hbm.1, f32[4,256]{1,0:T(4,128)} %rf_hbm.1, ...), custom_call_target="tpu_custom_call" | custom-call | tf_op jit(solution)/shard_map/step/pallas_call | solution.py:577
  93.2 3.3 %unpack.1 = (bf16[4,256,8,128]{3,2,1,0:T(8,128)(2,1)}, f32[64,256]{1,0:T(8,128)}, f32[9,64,64]{2,1,0:T(8,128)}, f32[64,256]{1,0:T(8,128)}, f32[4,256]{1,0:T(4,12...) custom-call(bf16[4,256,8,128]{3,2,1,0:T(8,128)(2,1)} %get-tuple-elem, ...), custom_call_target="tpu_custom_call" | custom-call | tf_op jit(solution)/shard_map/unpack/pallas_call | solution.py:646

commit v4 on v3

--- a/solution.py
+++ b/solution.py
@@ -15,13 +15,9 @@
 F32 = jnp.float32
 BF16 = jnp.bfloat16
 
-SHARE, WITH_PART = 40, 48
-REDUCE_F, OUTPUT_F, COLUMN_F, TILES = 36, 37, 38, 48
-NORMS = 16 * WITH_PART
-
-
-def other(t):
-    return t % 16, 16 + 8 * (t // 16)
+EARLY, LATE, WHOLE = 8, 16, 32
+OUTPUT_F, EXPAND_F, EARLY_TILES = 16, 17, 32
+SPATIAL, REDUCE_F, SPATIAL_F, LATE_TILES = 16, 52, 53, 64
 
 
 def dot(a, b, ca, cb):
@@ -41,21 +37,21 @@
     return s * (1.0 + v * (1.0 - s))
 
 
-def total(buf):
+def total(buf, n=16):
     t = buf[0]
-    for k in range(1, 16):
+    for k in range(1, n):
         t = t + buf[k]
     return t
 
 
 def kernel(
     x_hbm, c_hbm, rw_hbm, sw_hbm, ew_hbm, rf_hbm, sf_hbm, ef_hbm, of_hbm, g1_hbm, b1_hbm, g2_hbm, b2_hbm,
-    y_hbm, packed,
+    y_hbm, late_hbm, early_hbm, norms_hbm,
     xraw, craw, wide, rw, sw, ew, rf, sf, ef, of, g1, b1, g2, b2,
     w1, w2, w2b, w3, rwt,
     x, c, u, ulow, h2, hb, hq, dq, dpre1, nf, pk, pr, arb, ara,
-    acce, accr, accs, sxs, bn, bn1, bn2, bnc, g, r1, r2, r3, cols,
-    ld_sem, st_sem, s_sem, r_sem, hs_sem, hr_sem,
+    acce, accr, accs, sxs, bn, bn0, bn1, bn2, bnc, e, e0, e1, e2, e3, g, g0, g1_, g2_, g3, norms, cols,
+    ld_sem, st_sem, s_sem, r_sem, hs_sem, hr_sem, cs_sem, cr_sem,
 ):
     count = float(64 * 4096)
     x_hi, y = lax.axis_index("rows_0"), lax.axis_index("rows_1")
@@ -72,6 +68,9 @@
     def peer_b(d):
         b = lax.rem(rank_b + d, 16)
         return (x_hi, y, lax.div(b, 2), x_lo, lax.rem(b, 2))
+
+    def peer_z(d):
+        return (x_hi, y, lax.rem(z + d, 8), x_lo, core)
 
     def at(dr, dc):
         rr, cc = lax.rem(row + dr + 8, 8), lax.rem(col + dc + 32, 32)
@@ -100,23 +99,52 @@
     for side in sides:
         pl.semaphore_signal(barrier, inc=1, device_id=at(*side), device_id_type=MESH)
 
-    def exchange(stage, src, buf, rank, peer):
-        def copy(d):
-            return pltpu.make_async_remote_copy(
-                src_ref=src(d), dst_ref=buf.at[rank], send_sem=s_sem.at[stage, d],
-                recv_sem=r_sem.at[stage, d], device_id=peer(d), device_id_type=MESH,
-            )
-
+    def exchange(stage, src, buf, rank, peer, n=16):
         def start(d, _):
-            copy(d).start()
+            pltpu.make_async_remote_copy(
+                src_ref=src(d), dst_ref=buf.at[rank], send_sem=s_sem.at[stage],
+                recv_sem=r_sem.at[stage], device_id=peer(d), device_id_type=MESH,
+            ).start()
             return 0
 
-        def wait(d, _):
-            copy(d).wait()
-            return 0
-
-        lax.fori_loop(1, 16, start, 0)
-        return lambda: lax.fori_loop(1, 16, wait, 0)
+        lax.fori_loop(1, n, start, 0)
+        return together(buf.at[pl.ds(0, n - 1)], s_sem.at[stage], r_sem.at[stage]).wait
+
+    def together(ref, send, recv):
+        return pltpu.make_async_remote_copy(
+            src_ref=ref, dst_ref=ref, send_sem=send, recv_sem=recv,
+            device_id=(x_hi, y, z, x_lo, 1 - core), device_id_type=MESH,
+        )
+
+    def swap(stage, src, dst):
+        copy = pltpu.make_async_remote_copy(
+            src_ref=src, dst_ref=dst, send_sem=cs_sem.at[stage], recv_sem=cr_sem.at[stage],
+            device_id=(x_hi, y, z, x_lo, 1 - core), device_id_type=MESH,
+        )
+        copy.start()
+        return copy.wait
+
+    def share_cores(stage, tiles, partner):
+        return swap(stage, tiles.at[1 - core], partner)
+
+    def share_plane(stage, wait, tiles, partner, buf):
+        wait()
+        for a in range(16):
+            partner[a] = partner[a] + tiles[core, a]
+        return exchange(stage, lambda d: partner.at[lax.rem(rank_a + d, 16)], buf, rank_a, peer_a)
+
+    def share_depth(stage, wait, partner, buf, slots):
+        wait()
+        buf[rank_a] = partner[rank_a]
+        slots[z] = total(buf)
+        return exchange(stage, lambda d: slots.at[z], slots, z, peer_z, 8)
+
+    def gather_plane(stage, whole):
+        return exchange(stage, lambda d: whole.at[core, rank_a], whole.at[core], rank_a, peer_a)
+
+    def gather_cores(stage, wait, whole):
+        wait()
+        return swap(stage, whole.at[core], whole.at[core])
 
     def sum_start(k, n, tile):
         arb[2 * k + n, rank_b] = tile
@@ -137,30 +165,34 @@
 
     def halo(k, n):
         members = pl.ds(2 * n, 2)
+        t = 2 * k + n
         copies = [
             pltpu.make_async_remote_copy(
                 src_ref=hb.at[k, members, :, pl.ds(128, 128)],
                 dst_ref=hb.at[k, members, :, pl.ds(1152, 128)],
-                send_sem=hs_sem.at[2 * k + n, 6], recv_sem=hr_sem.at[2 * k + n, 6],
+                send_sem=hs_sem.at[t, 0], recv_sem=hr_sem.at[t, 0],
                 device_id=at(-1, 0), device_id_type=MESH,
             ),
             pltpu.make_async_remote_copy(
                 src_ref=hb.at[k, members, :, pl.ds(1024, 128)],
                 dst_ref=hb.at[k, members, :, pl.ds(0, 128)],
-                send_sem=hs_sem.at[2 * k + n, 7], recv_sem=hr_sem.at[2 * k + n, 7],
+                send_sem=hs_sem.at[t, 0], recv_sem=hr_sem.at[t, 0],
                 device_id=at(1, 0), device_id_type=MESH,
             ),
         ]
-        for e, side in enumerate(sides):
+        for edge, side in enumerate(sides):
             copies.append(
                 pltpu.make_async_remote_copy(
-                    src_ref=pk.at[k, n], dst_ref=pr.at[k, n, e], send_sem=hs_sem.at[2 * k + n, e],
-                    recv_sem=hr_sem.at[2 * k + n, e], device_id=at(*side), device_id_type=MESH,
+                    src_ref=pk.at[k, n], dst_ref=pr.at[k, n, edge], send_sem=hs_sem.at[t, 1],
+                    recv_sem=hr_sem.at[t, 1], device_id=at(*side), device_id_type=MESH,
                 )
             )
         for copy in copies:
             copy.start()
-        return copies
+        return [
+            together(hb.at[k, :, :, pl.ds(0, 128)], hs_sem.at[t, 0], hr_sem.at[t, 0]),
+            together(pr.at[k, n], hs_sem.at[t, 1], hr_sem.at[t, 1]),
+        ]
 
     lane = lax.broadcasted_iota(jnp.int32, (64, 128), 1)
     sub = lax.broadcasted_iota(jnp.int32, (8, 128), 0)
@@ -247,7 +279,7 @@
         base = 2 if m < 2 else 0
         return (base + 4 * (m % 2), base + 4 * (m % 2) + 1)
 
-    stats, halos = [None, None], [None, None]
+    stats, halos, tiles = [None, None], [None, None], [None, None]
     for n in range(2):
         acc = zero
         extra = []
@@ -258,14 +290,15 @@
             hb[0, m, :, 128:1152] = a
             acc = sums(m, acc, a, a * a)
             extra.append((m, dot(ones, x[m], 1, 1)))
+        tile = rows_of_columns(acc)
+        for m, line in extra:
+            for h, r in enumerate(free_rows(m)):
+                tile = jnp.where(sub == r, line[:, h * 128 : h * 128 + 128], tile)
+        tiles[n] = tile
         pack(0, n)
-        tile = rows_of_columns(acc)
-        for m, e in extra:
-            for h, r in enumerate(free_rows(m)):
-                tile = jnp.where(sub == r, e[:, h * 128 : h * 128 + 128], tile)
-        if n == 0:
-            pl.semaphore_wait(barrier, 36)
-        stats[n] = sum_start(0, n, tile)
+    pl.semaphore_wait(barrier, 36)
+    for n in range(2):
+        stats[n] = sum_start(0, n, tiles[n])
         halos[n] = halo(0, n)
 
     for copy in load_w[2:]:
@@ -290,11 +323,9 @@
     gain1, shift1, gain2, shift2 = (cols[10, n] for n in range(4))
     for copy in load_c:
         copy.wait()
-    for m in range(2):
+    for m in range(4):
         flatten(craw, c, m)
     stats[0] = sum_middle(0, 0, stats[0])
-    for m in range(2, 4):
-        flatten(craw, c, m)
     stats[1] = sum_middle(0, 1, stats[1])
 
     for n in range(2):
@@ -321,8 +352,8 @@
             a = a + dot(w2[m, 2], hq[m, :, 256:1280], 0, 0)
             hb[1, m, :, 128:1152] = a
             acc = sums(m, acc, a, a * a)
+        stats[n] = sum_start(1, n, rows_of_columns(acc))
         pack(1, n)
-        stats[n] = sum_start(1, n, rows_of_columns(acc))
         halos[n] = halo(1, n)
 
     def project(m):
@@ -330,15 +361,14 @@
         part = dot(normed, x[m], 1, 1)
         for a in range(16):
             h, f = a // 8, a % 8
-            bn[a, m * 8 : m * 8 + 8] = part[f * 8 : f * 8 + 8, h * 128 : h * 128 + 128]
-
-    project(0)
-    project(1)
+            bn[m // 2, a, m % 2 * 8 : m % 2 * 8 + 8] = part[f * 8 : f * 8 + 8, h * 128 : h * 128 + 128]
+
+    for m in range(4):
+        project(m)
+    corrections = share_cores(0, bn, bn0)
     stats[0] = sum_middle(1, 0, stats[0])
-    project(2)
-    project(3)
     stats[1] = sum_middle(1, 1, stats[1])
-    features = exchange(16, lambda d: bn.at[lax.rem(rank_a + d, 16)], bn1, rank_a, peer_a)
+    corrections = share_plane(16, corrections, bn, bn0, bn1)
 
     sums2 = []
     for n in range(2):
@@ -362,8 +392,8 @@
             hb[2, m, :, 128:1152] = back
             dpre = back * dpre1[m]
             acc = sums(m, acc, dpre, dpre * ((hb[1, m, :, 128:1152] - mean) * rstd))
+        stats[n] = sum_start(2, n, rows_of_columns(acc))
         pack(2, n)
-        stats[n] = sum_start(2, n, rows_of_columns(acc))
         halos[n] = halo(2, n)
 
     fac = zero
@@ -377,14 +407,30 @@
         nf[1, m] = jnp.sum(byw * efm, axis=0, keepdims=True)
         return put(fac, m, jnp.sum(byw * ofm, axis=1, keepdims=True))
 
-    fac = expand(1, expand(0, fac))
+    for m in range(4):
+        fac = expand(m, fac)
+
+    def place(buf, t, value):
+        r = t // 32 * 8
+        buf[t // 16 % 2, t % 16, r : r + 8] = value
+
+    def lines(k):
+        return jnp.concatenate(
+            [nf[k, m, :, h * 128 : h * 128 + 128] for h in range(2) for m in range(4)], axis=0
+        )
+
+    for a in range(16):
+        h, f = a // 8, a % 8
+        place(e, a, acce[f * 8 : f * 8 + 8, h * 128 : h * 128 + 128])
+    place(e, OUTPUT_F, lines(1))
+    place(e, EXPAND_F, rows_of_columns(fac))
+    for t in range(EXPAND_F + 1, EARLY_TILES):
+        place(e, t, jnp.zeros((8, 128), F32))
+    early = share_cores(1, e, e0)
     stats[0] = sum_middle(2, 0, stats[0])
-    fac = expand(3, expand(2, fac))
     stats[1] = sum_middle(2, 1, stats[1])
-    features()
-    bn1[rank_a] = bn[rank_a]
-    bn2[rank_b] = total(bn1)
-    features = exchange(17, lambda d: bn2.at[rank_b], bn2, rank_b, peer_b)
+    early = share_plane(18, early, e, e0, e1)
+    corrections = share_depth(17, corrections, bn0, bn1, bn2)
 
     for n in range(2):
         tile = sum_end(2, n, stats[n])
@@ -430,35 +476,33 @@
         scaled = part * rf[m : m + 1]
         accr[...] = scaled if m == 0 else accr[...] + scaled
         nf[0, m] = jnp.sum(part * rwt[...], axis=0, keepdims=True)
-        return put(fac, 4 + m, byf)
-
-    fac = gradients(1, gradients(0, fac))
-    stats[0] = sum_middle(3, 0, stats[0])
-    fac = gradients(3, gradients(2, fac))
-    stats[1] = sum_middle(3, 1, stats[1])
+        return put(fac, m, byf)
+
+    fac = zero
+    for m in range(4):
+        fac = gradients(m, fac)
     for a in range(16):
         h, f = a // 8, a % 8
-        g[a, 0:8] = acce[f * 8 : f * 8 + 8, h * 128 : h * 128 + 128]
-        g[a, 8:16] = accr[f * 8 : f * 8 + 8, h * 128 : h * 128 + 128]
+        place(g, a, accr[f * 8 : f * 8 + 8, h * 128 : h * 128 + 128])
     for t in range(36):
         low, high = t * 8, 288 + t * 8
-        a, r = other(t)
-        g[a, r : r + 8] = jnp.concatenate(
+        place(g, SPATIAL + t, jnp.concatenate(
             [accs[low // 64, low % 64 : low % 64 + 8], accs[high // 64, high % 64 : high % 64 + 8]], axis=1
-        )
-    for k, t in ((0, REDUCE_F), (1, OUTPUT_F)):
-        a, r = other(t)
-        g[a, r : r + 8] = jnp.concatenate(
-            [nf[k, m, :, h * 128 : h * 128 + 128] for h in range(2) for m in range(4)], axis=0
-        )
-    a, r = other(COLUMN_F)
-    g[a, r : r + 8] = rows_of_columns(fac)
-    for t in range(COLUMN_F + 1, TILES):
-        a, r = other(t)
-        g[a, r : r + 8] = jnp.zeros((8, 128), F32)
-    shares = exchange(18, lambda d: g.at[lax.rem(rank_a + d, 16)], r1, rank_a, peer_a)
-    features()
-    bnc[...] = total(bn2)
+        ))
+    place(g, REDUCE_F, lines(0))
+    place(g, SPATIAL_F, rows_of_columns(fac))
+    for t in range(SPATIAL_F + 1, LATE_TILES):
+        place(g, t, jnp.zeros((8, 128), F32))
+    late = share_cores(2, g, g0)
+    early = share_depth(19, early, e0, e1, e2)
+    late = share_plane(21, late, g, g0, g1_)
+    stats[0] = sum_middle(3, 0, stats[0])
+    stats[1] = sum_middle(3, 1, stats[1])
+    corrections()
+    bnc[...] = total(bn2, 8)
+    early()
+    e3[core, rank_a] = total(e2, 8)
+    early = gather_plane(20, e3)
 
     def finish(m):
         mean, rstd, plain, weighted = cols[0, m], cols[1, m], cols[6, m] / count, cols[7, m] / count
@@ -477,38 +521,35 @@
     tile = sum_end(3, 0, stats[0])
     sums1 = [tile]
     columns_of_rows(tile, 6, group(0))
+    late = share_depth(22, late, g0, g1_, g2_)
     stores = [finish(0), finish(1)]
-    shares()
-    r1[rank_a] = g[rank_a]
-    r2[rank_b] = total(r1)
-    shares = exchange(19, lambda d: r2.at[rank_b], r2, rank_b, peer_b)
     tile = sum_end(3, 1, stats[1])
     sums1.append(tile)
     columns_of_rows(tile, 6, group(1))
-    stores += [finish(2), finish(3)]
 
     half, block = lax.div(rank_a, 8), pl.ds(pl.multiple_of(lax.rem(rank_a, 8) * 8, 8), 8)
     span = pl.ds(pl.multiple_of(half * 128, 128), 128)
     fix = jnp.zeros((8, 128), F32)
     part = jnp.zeros((8, 128), F32)
-    for m in range(4):
+    for k in range(2):
+        m = 2 * core + k
         plain, weighted = cols[6, m, block] / count, cols[7, m, block] / count
-        e = cols[10, 0, block] * cols[1, m, block] * (
-            plain * sxs[m, half] + weighted * bnc[m * 8 : m * 8 + 8]
+        v = cols[10, 0, block] * cols[1, m, block] * (
+            plain * sxs[m, half] + weighted * bnc[k * 8 : k * 8 + 8]
         )
-        fix = fix + e * rf[m : m + 1, span]
+        fix = fix + v * jnp.where(core == 0, rf[k : k + 1, span], rf[k + 2 : k + 3, span])
         part = jnp.where(
-            sub == half * 4 + m, jnp.sum(e * rwt[block, span], axis=0, keepdims=True), part
+            sub == half * 4 + m, jnp.sum(v * rwt[block, span], axis=0, keepdims=True), part
         )
-    shares()
-    share = total(r2)
-    r3[rank_a, 0:8] = share[0:8]
-    r3[rank_a, 8:16] = share[8:16] - fix
-    r3[rank_a, 16:40] = share[16:40]
-    r3[rank_a, 40:48] = part
-    shares = exchange(20, lambda d: r3.at[rank_a], r3, rank_a, peer_a)
+    g3[core, rank_a, LATE : LATE + 8] = fix
+    g3[core, rank_a, LATE + 8 : WHOLE] = part
+    late()
+    g3[core, rank_a, 0:LATE] = total(g2_, 8)
+    late = gather_plane(23, g3)
+    early = gather_cores(3, early, e3)
+    stores += [finish(2), finish(3)]
     first, second = sums1[0] + sums1[1], sums2[0] + sums2[1]
-    packed[NORMS : NORMS + 8] = jnp.concatenate(
+    norms[...] = jnp.concatenate(
         [
             jnp.sum(first[4:8], axis=0, keepdims=True),
             jnp.sum(first[0:4], axis=0, keepdims=True),
@@ -518,50 +559,66 @@
         ],
         axis=0,
     )
-    shares()
-    for a in range(16):
-        packed[a * WITH_PART : a * WITH_PART + WITH_PART] = r3[a]
+    stores.append(pltpu.make_async_copy(norms, norms_hbm, st_sem.at[4]))
+    stores[-1].start()
+    late = gather_cores(4, late, g3)
+    early()
+    stores.append(pltpu.make_async_copy(e3, early_hbm, st_sem.at[5]))
+    stores[-1].start()
+    late()
+    stores.append(pltpu.make_async_copy(g3, late_hbm, st_sem.at[6]))
+    stores[-1].start()
     for copy in stores:
         copy.wait()
 
 
 def unpack(
-    y_hbm, packed_hbm,
+    y_hbm, late_hbm, early_hbm, norms_hbm,
     out_hbm, o_reduce, o_spatial, o_expand, o_rf, o_sf, o_ef, o_of, o_g1, o_b1, o_g2, o_b2,
-    y, packed, sem,
+    y, whole, expand, norms, sem,
 ):
-    load = [pltpu.make_async_copy(packed_hbm, packed, sem.at[0])]
-    load += [pltpu.make_async_copy(y_hbm.at[m], y.at[m], sem.at[1 + m]) for m in range(4)]
-    store = [pltpu.make_async_copy(y.at[m], out_hbm.at[m], sem.at[5 + m]) for m in range(4)]
-    for copy in load:
+    load = [pltpu.make_async_copy(y_hbm.at[m], y.at[m], sem.at[m]) for m in range(4)]
+    store = [pltpu.make_async_copy(y.at[m], out_hbm.at[m], sem.at[4 + m]) for m in range(4)]
+    small = [
+        pltpu.make_async_copy(src, dst, sem.at[8 + n])
+        for n, (src, dst) in enumerate(((late_hbm, whole), (early_hbm, expand), (norms_hbm, norms)))
+    ]
+    for copy in load + small:
         copy.start()
     for m in range(4):
-        load[1 + m].wait()
+        load[m].wait()
         store[m].start()
-    load[0].wait()
-
-    def tile(a, r):
-        return packed[a * WITH_PART + r : a * WITH_PART + r + 8]
+    for copy in small:
+        copy.wait()
+
+    def early(t):
+        return expand[t // 16, t % 16]
+
+    def late(t):
+        return whole[t // 16 % 2, t % 16, t // 32 * 8 : t // 32 * 8 + 8]
+
+    def fixes(a, k):
+        r = LATE + k * 8
+        return whole[0, a, r : r + 8] + whole[1, a, r : r + 8]
 
     fix = jnp.zeros((8, 128), F32)
     for a in range(16):
         h, f = a // 8, a % 8
-        o_expand[f * 8 : f * 8 + 8, h * 128 : h * 128 + 128] = tile(a, 0)
-        o_reduce[f * 8 : f * 8 + 8, h * 128 : h * 128 + 128] = tile(a, 8)
-        fix = fix + tile(a, 40)
+        o_expand[f * 8 : f * 8 + 8, h * 128 : h * 128 + 128] = early(a)
+        o_reduce[f * 8 : f * 8 + 8, h * 128 : h * 128 + 128] = late(a) - fixes(a, 0)
+        fix = fix + fixes(a, 1)
     for t in range(36):
-        both = tile(*other(t))
+        both = late(SPATIAL + t)
         for n in range(2):
             r = n * 288 + t * 8
             o_spatial[r // 64, r % 64 : r % 64 + 8] = both[:, n * 64 : n * 64 + 64]
-    for o, e in ((o_rf, tile(*other(REDUCE_F)) - fix), (o_of, tile(*other(OUTPUT_F)))):
+    for o, e in ((o_rf, late(REDUCE_F) - fix), (o_of, early(OUTPUT_F))):
         o[:, :128] = e[:4]
         o[:, 128:] = e[4:]
-    e = tile(*other(COLUMN_F))
-    o_ef[...] = e[:4, :64]
-    o_sf[...] = e[4:, :64]
+    o_ef[...] = early(EXPAND_F)[:4, :64]
+    o_sf[...] = late(SPATIAL_F)[:4, :64]
     for n, o in enumerate((o_g1, o_b1, o_g2, o_b2)):
-        o[...] = packed[NORMS + n : NORMS + n + 1, :64]
+        o[...] = norms[n : n + 1, :64]
     for copy in store:
         copy.wait()
 
@@ -574,11 +631,14 @@
     vmem = pl.BlockSpec(memory_space=pltpu.VMEM)
     hbm = pl.BlockSpec(memory_space=pl.ANY)
     sds = jax.ShapeDtypeStruct
-    y, packed = pl.pallas_call(
+    bufs = pl.pallas_call(
         kernel,
-        out_shape=(sds((4, 256, 8, 128), BF16), sds((NORMS + 8, 128), F32)),
+        out_shape=(
+            sds((4, 256, 8, 128), BF16), sds((2, 16, WHOLE, 128), F32), sds((2, 16, EARLY, 128), F32),
+            sds((8, 128), F32),
+        ),
         in_specs=[hbm] * 13,
-        out_specs=(hbm, vmem),
+        out_specs=(hbm,) * 4,
         scratch_shapes=[
             pltpu.VMEM((4, 256, 8, 128), BF16),
             pltpu.VMEM((4, 256, 8, 128), BF16),
@@ -617,21 +677,31 @@
             pltpu.VMEM((64, 256), F32),
             pltpu.VMEM((9, 64, 64), F32),
             pltpu.VMEM((4, 2, 8, 128), F32),
-            pltpu.VMEM((16, 32, 128), F32),
-            pltpu.VMEM((16, 32, 128), F32),
-            pltpu.VMEM((16, 32, 128), F32),
-            pltpu.VMEM((32, 128), F32),
-            pltpu.VMEM((16, SHARE, 128), F32),
-            pltpu.VMEM((16, SHARE, 128), F32),
-            pltpu.VMEM((16, SHARE, 128), F32),
-            pltpu.VMEM((16, WITH_PART, 128), F32),
+            pltpu.VMEM((2, 16, 16, 128), F32),
+            pltpu.VMEM((16, 16, 128), F32),
+            pltpu.VMEM((16, 16, 128), F32),
+            pltpu.VMEM((8, 16, 128), F32),
+            pltpu.VMEM((16, 128), F32),
+            pltpu.VMEM((2, 16, EARLY, 128), F32),
+            pltpu.VMEM((16, EARLY, 128), F32),
+            pltpu.VMEM((16, EARLY, 128), F32),
+            pltpu.VMEM((8, EARLY, 128), F32),
+            pltpu.VMEM((2, 16, EARLY, 128), F32),
+            pltpu.VMEM((2, 16, LATE, 128), F32),
+            pltpu.VMEM((16, LATE, 128), F32),
+            pltpu.VMEM((16, LATE, 128), F32),
+            pltpu.VMEM((8, LATE, 128), F32),
+            pltpu.VMEM((2, 16, WHOLE, 128), F32),
+            pltpu.VMEM((8, 128), F32),
             pltpu.VMEM((12, 4, 64, 1), F32),
             pltpu.SemaphoreType.DMA((20,)),
-            pltpu.SemaphoreType.DMA((4,)),
-            pltpu.SemaphoreType.DMA((21, 16)),
-            pltpu.SemaphoreType.DMA((21, 16)),
-            pltpu.SemaphoreType.DMA((6, 8)),
-            pltpu.SemaphoreType.DMA((6, 8)),
+            pltpu.SemaphoreType.DMA((7,)),
+            pltpu.SemaphoreType.DMA((24,)),
+            pltpu.SemaphoreType.DMA((24,)),
+            pltpu.SemaphoreType.DMA((6, 2)),
+            pltpu.SemaphoreType.DMA((6, 2)),
+            pltpu.SemaphoreType.DMA((5,)),
+            pltpu.SemaphoreType.DMA((5,)),
         ],
         compiler_params=pltpu.CompilerParams(
             collective_id=0, has_side_effects=True, vmem_limit_bytes=67043328
@@ -649,16 +719,18 @@
             sds((4, 256, 8, 128), BF16), sds((64, 256), F32), sds((9, 64, 64), F32), sds((64, 256), F32),
             sds((4, 256), F32), sds((4, 64), F32), sds((4, 64), F32), sds((4, 256), F32),
         ) + (sds((1, 64), F32),) * 4,
-        in_specs=[hbm, hbm],
+        in_specs=[hbm] * 4,
         out_specs=(hbm,) + (vmem,) * 11,
         scratch_shapes=[
             pltpu.VMEM((4, 256, 8, 128), BF16),
-            pltpu.VMEM((NORMS + 8, 128), F32),
-            pltpu.SemaphoreType.DMA((9,)),
+            pltpu.VMEM((2, 16, WHOLE, 128), F32),
+            pltpu.VMEM((2, 16, EARLY, 128), F32),
+            pltpu.VMEM((8, 128), F32),
+            pltpu.SemaphoreType.DMA((11,)),
         ],
         compiler_params=pltpu.CompilerParams(vmem_limit_bytes=67043328),
         name="unpack",
-    )(y, packed)
+    )(*bufs)
     return (outs[0], outs[1].T) + outs[2:8] + tuple(o.reshape(64) for o in outs[8:])
 
 

time: 96.9 us -> 83.2 us (0.86)
  Pallas kernels: 95.9 us -> 82.3 us
    pallas_call x1, Pallas kernels: 92.6 us -> 79 us  [body(): pl.pallas_call(kernel, out_shape=(sds((4, 256, 8, 128), BF16), sds((2, 16...]
where the time goes in v4:
time: 83.2 us; the launch traced here: 83.1 us
  Pallas kernels  82.3 us (99%)
    pallas_call x1, Pallas kernels, body(): pl.pallas_call(kernel, out_shape=(sds((4, 256, 8, 128), BF16), sds((2, 16...  79 us
    pallas_call x1, Pallas kernels, body(): pl.pallas_call(unpack, out_shape=(sds((4, 256, 8, 128), BF16), sds((64, 2...  3.22 us

profile of v4, /device:TPU:1, one launch (start us, length us, event | category | flops | bytes accessed | tf_op | source)
XLA Modules:
  0.0 83.1 jit_solution(8229057185311704075)
XLA Ops:
  0.6 79.0 %step.1 = (bf16[4,256,8,128]{3,2,1,0:T(8,128)(2,1)}, f32[2,16,32,128]{3,2,1,0:T(8,128)}, f32[2,16,8,128]{3,2,1,0:T(8,128)}, f32[8,128]{1,0:T(8,128)}) custom-call(bf16[4,256,8,128]{3,2,1,0:T(8,128)(2,1)} %x_hbm.1, bf16[4,256,8,128]{3,2,1,0:T(8,128)(2,1)} %c_hbm.1, bf16[64,256]{1,0:T(8,128)(2,1)} %bitcast.10, bf16[9,64,64]{2,1,0:T(8,128)(2,1)} %sw_hbm.1, ...), custom_call_target="tpu_custom_call" | custom-call | tf_op jit(solution)/shard_map/step/pallas_call | solution.py:634
  79.7 3.2 %unpack.1 = (bf16[4,256,8,128]{3,2,1,0:T(8,128)(2,1)}, f32[64,256]{1,0:T(8,128)}, f32[9,64,64]{2,1,0:T(8,128)}, f32[64,256]{1,0:T(8,128)}, f32[4,256]{1,0:T(4,12...) custom-call(bf16[4,256,8,128]{3,2,1,0:T(8,128)(2,1)} %get-tuple-elem, ...), custom_call_target="tpu_custom_call" | custom-call | tf_op jit(solution)/shard_map/unpack/pallas_call | solution.py:716

commit v5 on v4

--- a/solution.py
+++ b/solution.py
@@ -15,7 +15,7 @@
 F32 = jnp.float32
 BF16 = jnp.bfloat16
 
-EARLY, LATE, WHOLE = 8, 16, 32
+EARLY, LATE, WHOLE = 8, 16, 24
 OUTPUT_F, EXPAND_F, EARLY_TILES = 16, 17, 32
 SPATIAL, REDUCE_F, SPATIAL_F, LATE_TILES = 16, 52, 53, 64
 
@@ -46,11 +46,11 @@
 
 def kernel(
     x_hbm, c_hbm, rw_hbm, sw_hbm, ew_hbm, rf_hbm, sf_hbm, ef_hbm, of_hbm, g1_hbm, b1_hbm, g2_hbm, b2_hbm,
-    y_hbm, late_hbm, early_hbm, norms_hbm,
+    y_hbm, late_out, early_out, norms,
     xraw, craw, wide, rw, sw, ew, rf, sf, ef, of, g1, b1, g2, b2,
     w1, w2, w2b, w3, rwt,
     x, c, u, ulow, h2, hb, hq, dq, dpre1, nf, pk, pr, arb, ara,
-    acce, accr, accs, sxs, bn, bn0, bn1, bn2, bnc, e, e0, e1, e2, e3, g, g0, g1_, g2_, g3, norms, cols,
+    acce, accr, accs, sxs, bn, bn0, bn1, bn2, bnc, e, e0, e1, e2, e3, g, g0, g1_, g2_, g3, both, slope1, ep, cols,
     ld_sem, st_sem, s_sem, r_sem, hs_sem, hr_sem, cs_sem, cr_sem,
 ):
     count = float(64 * 4096)
@@ -78,6 +78,17 @@
 
     sides = ((0, 1), (0, -1), (1, 1), (1, -1), (-1, 1), (-1, -1))
 
+    barrier = pltpu.get_barrier_semaphore()
+
+    def greet(d, _):
+        pl.semaphore_signal(barrier, inc=1, device_id=peer_a(d), device_id_type=MESH)
+        pl.semaphore_signal(barrier, inc=1, device_id=peer_b(d), device_id_type=MESH)
+        return 0
+
+    lax.fori_loop(1, 16, greet, 0)
+    for side in sides:
+        pl.semaphore_signal(barrier, inc=1, device_id=at(*side), device_id_type=MESH)
+
     pairs = (
         (rw_hbm, rw), (rf_hbm, rf), (sw_hbm, sw), (ew_hbm, ew), (sf_hbm, sf), (ef_hbm, ef), (of_hbm, of),
         (g1_hbm, g1), (b1_hbm, b1), (g2_hbm, g2), (b2_hbm, b2),
@@ -87,17 +98,6 @@
     load_c = [pltpu.make_async_copy(c_hbm.at[m], craw.at[m], ld_sem.at[4 + m]) for m in range(4)]
     for copy in load_w[:2] + load_x + load_w[2:] + load_c:
         copy.start()
-
-    barrier = pltpu.get_barrier_semaphore()
-
-    def greet(d, _):
-        pl.semaphore_signal(barrier, inc=1, device_id=peer_a(d), device_id_type=MESH)
-        pl.semaphore_signal(barrier, inc=1, device_id=peer_b(d), device_id_type=MESH)
-        return 0
-
-    lax.fori_loop(1, 16, greet, 0)
-    for side in sides:
-        pl.semaphore_signal(barrier, inc=1, device_id=at(*side), device_id_type=MESH)
 
     def exchange(stage, src, buf, rank, peer, n=16):
         def start(d, _):
@@ -279,7 +279,7 @@
         base = 2 if m < 2 else 0
         return (base + 4 * (m % 2), base + 4 * (m % 2) + 1)
 
-    stats, halos, tiles = [None, None], [None, None], [None, None]
+    stats, halos = [None, None], [None, None]
     for n in range(2):
         acc = zero
         extra = []
@@ -294,11 +294,10 @@
         for m, line in extra:
             for h, r in enumerate(free_rows(m)):
                 tile = jnp.where(sub == r, line[:, h * 128 : h * 128 + 128], tile)
-        tiles[n] = tile
+        if n == 0:
+            pl.semaphore_wait(barrier, 36)
+        stats[n] = sum_start(0, n, tile)
         pack(0, n)
-    pl.semaphore_wait(barrier, 36)
-    for n in range(2):
-        stats[n] = sum_start(0, n, tiles[n])
         halos[n] = halo(0, n)
 
     for copy in load_w[2:]:
@@ -357,8 +356,9 @@
         halos[n] = halo(1, n)
 
     def project(m):
-        normed = ((hb[0, m, :, 128:1152] - cols[0, m]) * cols[1, m]).astype(BF16)
-        part = dot(normed, x[m], 1, 1)
+        normed = (hb[0, m, :, 128:1152] - cols[0, m]) * cols[1, m]
+        slope1[m] = slope(gain1 * normed + shift1)
+        part = dot(normed.astype(BF16), x[m], 1, 1)
         for a in range(16):
             h, f = a // 8, a % 8
             bn[m // 2, a, m % 2 * 8 : m % 2 * 8 + 8] = part[f * 8 : f * 8 + 8, h * 128 : h * 128 + 128]
@@ -427,8 +427,28 @@
     for t in range(EXPAND_F + 1, EARLY_TILES):
         place(e, t, jnp.zeros((8, 128), F32))
     early = share_cores(1, e, e0)
+
+    def prepare(n):
+        for copy in halos[n]:
+            copy.wait()
+        for m in group(n):
+            mean, rstd = cols[2, m], cols[3, m]
+            scale = gain2 * rstd
+
+            def halves(second, back):
+                normed = (second - mean) * rstd
+                return scale * normed, scale * (back * slope(gain2 * normed + shift2))
+
+            for i in range(10):
+                span = slice(i * 128, i * 128 + 128)
+                hb[1, m, :, span], hb[2, m, :, span] = halves(hb[1, m, :, span], hb[2, m, :, span])
+            for edge in range(6):
+                ep[0, m, edge], ep[1, m, edge] = halves(pr[1, n, edge], pr[2, n, edge])
+
     stats[0] = sum_middle(2, 0, stats[0])
+    prepare(0)
     stats[1] = sum_middle(2, 1, stats[1])
+    prepare(1)
     early = share_plane(18, early, e, e0, e1)
     corrections = share_depth(17, corrections, bn0, bn1, bn2)
 
@@ -436,27 +456,23 @@
         tile = sum_end(2, n, stats[n])
         sums2.append(tile)
         columns_of_rows(tile, 4, group(n))
-        for copy in halos[n]:
-            copy.wait()
         acc = zero
         for m in group(n):
-            mean, rstd, plain, weighted = cols[2, m], cols[3, m], cols[4, m] / count, cols[5, m] / count
-
-            def dact(second, back):
-                normed = (second - mean) * rstd
-                dpre = back * slope(gain2 * normed + shift2)
-                return gain2 * rstd * (dpre - plain - normed * weighted)
+            plain, weighted = gain2 * cols[3, m] * cols[4, m] / count, cols[5, m] / count
+
+            def dact(normed, part):
+                return part - plain - normed * weighted
 
             spread(
                 dq, m,
                 lambda i: dact(hb[1, m, :, i * 128 : i * 128 + 128], hb[2, m, :, i * 128 : i * 128 + 128]),
-                lambda e: dact(pr[1, n, e], pr[2, n, e]),
+                lambda edge: dact(ep[0, m, edge], ep[1, m, edge]),
             )
             a = dot(w2b[m, 0], dq[m, :, 0:1024], 1, 0)
             a = a + dot(w2b[m, 1], dq[m, :, 128:1152], 1, 0)
             a = a + dot(w2b[m, 2], dq[m, :, 256:1280], 1, 0)
             normed = (hb[0, m, :, 128:1152] - cols[0, m]) * cols[1, m]
-            dpre = a * slope(gain1 * normed + shift1)
+            dpre = a * slope1[m]
             dpre1[m] = dpre
             acc = sums(m, acc, dpre, dpre * normed)
         stats[n] = sum_start(3, n, rows_of_columns(acc))
@@ -541,10 +557,15 @@
         part = jnp.where(
             sub == half * 4 + m, jnp.sum(v * rwt[block, span], axis=0, keepdims=True), part
         )
-    g3[core, rank_a, LATE : LATE + 8] = fix
-    g3[core, rank_a, LATE + 8 : WHOLE] = part
+    both[core, 0:8] = fix
+    both[core, 8:16] = part
+    swap(5, both.at[core], both.at[core])()
+    fix = jnp.where(core == 0, both[0, 0:8] + both[1, 0:8], 0.0)
     late()
-    g3[core, rank_a, 0:LATE] = total(g2_, 8)
+    share = total(g2_, 8)
+    g3[core, rank_a, 0:8] = share[0:8] - fix
+    g3[core, rank_a, 8:LATE] = share[8:LATE]
+    g3[core, rank_a, LATE:WHOLE] = both[0, 8:16] + both[1, 8:16]
     late = gather_plane(23, g3)
     early = gather_cores(3, early, e3)
     stores += [finish(2), finish(3)]
@@ -559,54 +580,36 @@
         ],
         axis=0,
     )
-    stores.append(pltpu.make_async_copy(norms, norms_hbm, st_sem.at[4]))
-    stores[-1].start()
     late = gather_cores(4, late, g3)
     early()
-    stores.append(pltpu.make_async_copy(e3, early_hbm, st_sem.at[5]))
-    stores[-1].start()
+    early_out[...] = e3[...]
     late()
-    stores.append(pltpu.make_async_copy(g3, late_hbm, st_sem.at[6]))
-    stores[-1].start()
+    late_out[...] = g3[...]
     for copy in stores:
         copy.wait()
 
 
 def unpack(
-    y_hbm, late_hbm, early_hbm, norms_hbm,
+    y_hbm, whole, expand, norms,
     out_hbm, o_reduce, o_spatial, o_expand, o_rf, o_sf, o_ef, o_of, o_g1, o_b1, o_g2, o_b2,
-    y, whole, expand, norms, sem,
+    sem,
 ):
-    load = [pltpu.make_async_copy(y_hbm.at[m], y.at[m], sem.at[m]) for m in range(4)]
-    store = [pltpu.make_async_copy(y.at[m], out_hbm.at[m], sem.at[4 + m]) for m in range(4)]
-    small = [
-        pltpu.make_async_copy(src, dst, sem.at[8 + n])
-        for n, (src, dst) in enumerate(((late_hbm, whole), (early_hbm, expand), (norms_hbm, norms)))
-    ]
-    for copy in load + small:
+    store = [pltpu.make_async_copy(y_hbm.at[m], out_hbm.at[m], sem.at[m]) for m in range(4)]
+    for copy in store:
         copy.start()
-    for m in range(4):
-        load[m].wait()
-        store[m].start()
-    for copy in small:
-        copy.wait()
 
     def early(t):
         return expand[t // 16, t % 16]
 
     def late(t):
         return whole[t // 16 % 2, t % 16, t // 32 * 8 : t // 32 * 8 + 8]
-
-    def fixes(a, k):
-        r = LATE + k * 8
-        return whole[0, a, r : r + 8] + whole[1, a, r : r + 8]
 
     fix = jnp.zeros((8, 128), F32)
     for a in range(16):
         h, f = a // 8, a % 8
         o_expand[f * 8 : f * 8 + 8, h * 128 : h * 128 + 128] = early(a)
-        o_reduce[f * 8 : f * 8 + 8, h * 128 : h * 128 + 128] = late(a) - fixes(a, 0)
-        fix = fix + fixes(a, 1)
+        o_reduce[f * 8 : f * 8 + 8, h * 128 : h * 128 + 128] = late(a)
+        fix = fix + whole[0, a, LATE:WHOLE]
     for t in range(36):
         both = late(SPATIAL + t)
         for n in range(2):
@@ -637,8 +640,8 @@
             sds((4, 256, 8, 128), BF16), sds((2, 16, WHOLE, 128), F32), sds((2, 16, EARLY, 128), F32),
             sds((8, 128), F32),
         ),
-        in_specs=[hbm] * 13,
-        out_specs=(hbm,) * 4,
+        in_specs=[pl.BlockSpec(memory_space=pltpu.HBM)] * 13,
+        out_specs=(hbm, vmem, vmem, vmem),
         scratch_shapes=[
             pltpu.VMEM((4, 256, 8, 128), BF16),
             pltpu.VMEM((4, 256, 8, 128), BF16),
@@ -692,43 +695,41 @@
             pltpu.VMEM((16, LATE, 128), F32),
             pltpu.VMEM((8, LATE, 128), F32),
             pltpu.VMEM((2, 16, WHOLE, 128), F32),
-            pltpu.VMEM((8, 128), F32),
+            pltpu.VMEM((2, 16, 128), F32),
+            pltpu.VMEM((4, 64, 1024), F32),
+            pltpu.VMEM((2, 4, 6, 64, 128), F32),
             pltpu.VMEM((12, 4, 64, 1), F32),
             pltpu.SemaphoreType.DMA((20,)),
-            pltpu.SemaphoreType.DMA((7,)),
+            pltpu.SemaphoreType.DMA((4,)),
             pltpu.SemaphoreType.DMA((24,)),
             pltpu.SemaphoreType.DMA((24,)),
             pltpu.SemaphoreType.DMA((6, 2)),
             pltpu.SemaphoreType.DMA((6, 2)),
-            pltpu.SemaphoreType.DMA((5,)),
-            pltpu.SemaphoreType.DMA((5,)),
+            pltpu.SemaphoreType.DMA((6,)),
+            pltpu.SemaphoreType.DMA((6,)),
         ],
         compiler_params=pltpu.CompilerParams(
-            collective_id=0, has_side_effects=True, vmem_limit_bytes=67043328
+            collective_id=0, has_side_effects=True, vmem_limit_bytes=44 * 1024 * 1024
         ),
         name="step",
-    )(
+    )(*[pltpu.with_memory_space_constraint(v, pltpu.HBM) for v in (
         features, cotangent, reduce_weight.T, spatial_weight, expand_weight,
         reduce_factor, spatial_factor, expand_factor, output_factor,
         gain_first.reshape(1, 64), shift_first.reshape(1, 64),
         gain_second.reshape(1, 64), shift_second.reshape(1, 64),
-    )
+    )])
     outs = pl.pallas_call(
         unpack,
         out_shape=(
             sds((4, 256, 8, 128), BF16), sds((64, 256), F32), sds((9, 64, 64), F32), sds((64, 256), F32),
             sds((4, 256), F32), sds((4, 64), F32), sds((4, 64), F32), sds((4, 256), F32),
         ) + (sds((1, 64), F32),) * 4,
-        in_specs=[hbm] * 4,
+        in_specs=[hbm, vmem, vmem, vmem],
         out_specs=(hbm,) + (vmem,) * 11,
         scratch_shapes=[
-            pltpu.VMEM((4, 256, 8, 128), BF16),
-            pltpu.VMEM((2, 16, WHOLE, 128), F32),
-            pltpu.VMEM((2, 16, EARLY, 128), F32),
-            pltpu.VMEM((8, 128), F32),
-            pltpu.SemaphoreType.DMA((11,)),
+            pltpu.SemaphoreType.DMA((4,)),
         ],
-        compiler_params=pltpu.CompilerParams(vmem_limit_bytes=67043328),
+        compiler_params=pltpu.CompilerParams(vmem_limit_bytes=8 * 1024 * 1024),
         name="unpack",
     )(*bufs)
     return (outs[0], outs[1].T) + outs[2:8] + tuple(o.reshape(64) for o in outs[8:])

time: 83.2 us -> 81.3 us (0.977)
  Pallas kernels: 82.3 us -> 80.4 us
    pallas_call x1, Pallas kernels: 3.22 us -> 2.13 us  [body(): pl.pallas_call(unpack, out_shape=(sds((4, 256, 8, 128), BF16), sds((64, 2...]
where the time goes in v5:
time: 81.3 us; the launch traced here: 81.2 us
  Pallas kernels  80.4 us (99%)
  between operations  0.82 us (1%)
    pallas_call x1, Pallas kernels, body(): pl.pallas_call(kernel, out_shape=(sds((4, 256, 8, 128), BF16), sds((2, 16...  78.2 us
    pallas_call x1, Pallas kernels, body(): pl.pallas_call(unpack, out_shape=(sds((4, 256, 8, 128), BF16), sds((64, 2...  2.13 us

profile of v5, /device:TPU:1, one launch (start us, length us, event | category | flops | bytes accessed | tf_op | source)
XLA Modules:
  0.0 81.2 jit_solution(10460459307222360219)
XLA Ops:
  0.6 78.2 %step.1 = (bf16[4,256,8,128]{3,2,1,0:T(8,128)(2,1)S(1)}, f32[2,16,24,128]{3,2,1,0:T(8,128)S(1)}, f32[2,16,8,128]{3,2,1,0:T(8,128)S(1)}, f32[8,128]{1,0:T(8,128)S(1)}) custom-call(bf16[4,256,8,128]{3,2,1,0:T(8,128)(2,1)} %x_hbm.1, bf16[4,256,8,128]{3,2,1,0:T(8,128)(2,1)} %c_hbm.1, bf16[64,256]{1,0:T(8,128)(2,1)} %bitcast.10, bf16[9,64,64]{2,1,0:T(8,128)(2,1)} %sw_hbm.1, ...), custom_call_target="tpu_custom_call" | custom-call | tf_op jit(solution)/shard_map/step/pallas_call | solution.py:637
  78.9 2.1 %unpack.1 = (bf16[4,256,8,128]{3,2,1,0:T(8,128)(2,1)}, f32[64,256]{1,0:T(8,128)}, f32[9,64,64]{2,1,0:T(8,128)}, f32[64,256]{1,0:T(8,128)}, f32[4,256]{1,0:T(4,12...) custom-call(bf16[4,256,8,128]{3,2,1,0:T(8,128)(2,1)S(1)} %get-tuple-, ...), custom_call_target="tpu_custom_call" | custom-call | tf_op jit(solution)/shard_map/unpack/pallas_call | solution.py:721

commit v6 on v5

--- a/solution.py
+++ b/solution.py
@@ -78,17 +78,6 @@
 
     sides = ((0, 1), (0, -1), (1, 1), (1, -1), (-1, 1), (-1, -1))
 
-    barrier = pltpu.get_barrier_semaphore()
-
-    def greet(d, _):
-        pl.semaphore_signal(barrier, inc=1, device_id=peer_a(d), device_id_type=MESH)
-        pl.semaphore_signal(barrier, inc=1, device_id=peer_b(d), device_id_type=MESH)
-        return 0
-
-    lax.fori_loop(1, 16, greet, 0)
-    for side in sides:
-        pl.semaphore_signal(barrier, inc=1, device_id=at(*side), device_id_type=MESH)
-
     pairs = (
         (rw_hbm, rw), (rf_hbm, rf), (sw_hbm, sw), (ew_hbm, ew), (sf_hbm, sf), (ef_hbm, ef), (of_hbm, of),
         (g1_hbm, g1), (b1_hbm, b1), (g2_hbm, g2), (b2_hbm, b2),
@@ -96,7 +85,20 @@
     load_w = [pltpu.make_async_copy(a, b, ld_sem.at[8 + n]) for n, (a, b) in enumerate(pairs)]
     load_x = [pltpu.make_async_copy(x_hbm.at[m], xraw.at[m], ld_sem.at[m]) for m in range(4)]
     load_c = [pltpu.make_async_copy(c_hbm.at[m], craw.at[m], ld_sem.at[4 + m]) for m in range(4)]
-    for copy in load_w[:2] + load_x + load_w[2:] + load_c:
+    for copy in load_w[:2] + load_x:
+        copy.start()
+
+    barrier = pltpu.get_barrier_semaphore()
+
+    def greet(d, _):
+        pl.semaphore_signal(barrier, inc=1, device_id=peer_a(d), device_id_type=MESH)
+        pl.semaphore_signal(barrier, inc=1, device_id=peer_b(d), device_id_type=MESH)
+        return 0
+
+    lax.fori_loop(1, 16, greet, 0)
+    for side in sides:
+        pl.semaphore_signal(barrier, inc=1, device_id=at(*side), device_id_type=MESH)
+    for copy in load_w[2:] + load_c:
         copy.start()
 
     def exchange(stage, src, buf, rank, peer, n=16):
@@ -183,7 +185,7 @@
         for edge, side in enumerate(sides):
             copies.append(
                 pltpu.make_async_remote_copy(
-                    src_ref=pk.at[k, n], dst_ref=pr.at[k, n, edge], send_sem=hs_sem.at[t, 1],
+                    src_ref=pk.at[k, n, (side[1] + 1) // 2], dst_ref=pr.at[k, n, edge], send_sem=hs_sem.at[t, 1],
                     recv_sem=hr_sem.at[t, 1], device_id=at(*side), device_id_type=MESH,
                 )
             )
@@ -219,9 +221,15 @@
         for m in group(n):
             for i in range(8):
                 t = hb[k, m, :, 128 + i * 128 : 256 + i * 128]
-                acc = put(acc, m * 8 + i, t[:, 0:1])
-                acc = put(acc, 32 + m * 8 + i, t[:, 127:128])
-        pk[k, n] = acc
+                acc = put(acc, m % 2 * 8 + i, t[:, 0:1])
+                acc = put(acc, 16 + m % 2 * 8 + i, t[:, 127:128])
+        t = jnp.transpose(jnp.concatenate([acc, zero], axis=0))
+        pk[k, n, 0] = t[0:16]
+        pk[k, n, 1] = t[16:32]
+
+    def received(k, n):
+        t = jnp.concatenate([pr[k, n, e] for e in range(6)] + [jnp.zeros((32, 128), F32)], axis=0)
+        return jnp.transpose(t)[:64]
 
     def group(n):
         return (2 * n, 2 * n + 1)
@@ -230,25 +238,26 @@
     bottom = jnp.where(row < 7, 1.0, 0.0).astype(F32)
     left = jnp.where(col > 0, 1.0, 0.0).astype(F32)
     right = jnp.where(col < 31, 1.0, 0.0).astype(F32)
-    masks = (left, right, top * left, top * right, bottom * left, bottom * right)
-
-    def spread(dst, m, tile, edge):
-        edges = [edge(e) * masks[e] for e in range(6)]
+    inside = zero
+    for edge, value in enumerate((left, right, top * left, top * right, bottom * left, bottom * right)):
+        inside = jnp.where((lane >= edge * 16) & (lane < edge * 16 + 16), value, inside)
+
+    def spread(dst, m, tile, edges):
+        edges = edges * inside
         for i in range(10):
             t = tile(i)
             if i == 0:
-                t, e0, e2, at_row = t * top, edges[2], edges[3], 7
+                t, first, at_row = t * top, 2, 7
             elif i == 9:
-                t, e0, e2, at_row = t * bottom, edges[4], edges[5], 0
+                t, first, at_row = t * bottom, 4, 0
             else:
-                e0, e2, at_row = edges[0], edges[1], i - 1
-            where0 = 32 + m * 8 + at_row
-            where2 = m * 8 + at_row
-            before = jnp.where(
-                lane == 0, pltpu.roll(e0, 128 - where0, axis=1), pltpu.roll(t, 1, axis=1)
-            )
+                first, at_row = 0, i - 1
+            where0 = first * 16 + m % 2 * 8 + at_row
+            where2 = where0 + 16
+            e0 = edges if where0 == 0 else pltpu.roll(edges, 128 - where0, axis=1)
+            before = jnp.where(lane == 0, e0, pltpu.roll(t, 1, axis=1))
             after = jnp.where(
-                lane == 127, pltpu.roll(e2, 127 - where2, axis=1), pltpu.roll(t, 127, axis=1)
+                lane == 127, pltpu.roll(edges, 127 - where2, axis=1), pltpu.roll(t, 127, axis=1)
             )
             span = slice(i * 128, i * 128 + 128)
             dst[m, 0:64, span] = before.astype(BF16)
@@ -335,6 +344,7 @@
                 sxs[m, h] = jnp.broadcast_to(tile[r : r + 1], (8, 128))
         for copy in halos[n]:
             copy.wait()
+        edges = received(0, n)
         acc = zero
         for m in group(n):
             mean, rstd = cols[0, m], cols[1, m]
@@ -344,7 +354,7 @@
 
             spread(
                 hq, m, lambda i: hidden(hb[0, m, :, i * 128 : i * 128 + 128]),
-                lambda e: hidden(pr[0, n, e]),
+                hidden(edges),
             )
             a = dot(w2[m, 0], hq[m, :, 0:1024], 0, 0)
             a = a + dot(w2[m, 1], hq[m, :, 128:1152], 0, 0)
@@ -431,6 +441,7 @@
     def prepare(n):
         for copy in halos[n]:
             copy.wait()
+        second_edges, back_edges = received(1, n), received(2, n)
         for m in group(n):
             mean, rstd = cols[2, m], cols[3, m]
             scale = gain2 * rstd
@@ -442,8 +453,7 @@
             for i in range(10):
                 span = slice(i * 128, i * 128 + 128)
                 hb[1, m, :, span], hb[2, m, :, span] = halves(hb[1, m, :, span], hb[2, m, :, span])
-            for edge in range(6):
-                ep[0, m, edge], ep[1, m, edge] = halves(pr[1, n, edge], pr[2, n, edge])
+            ep[0, m], ep[1, m] = halves(second_edges, back_edges)
 
     stats[0] = sum_middle(2, 0, stats[0])
     prepare(0)
@@ -466,7 +476,7 @@
             spread(
                 dq, m,
                 lambda i: dact(hb[1, m, :, i * 128 : i * 128 + 128], hb[2, m, :, i * 128 : i * 128 + 128]),
-                lambda edge: dact(ep[0, m, edge], ep[1, m, edge]),
+                dact(ep[0, m], ep[1, m]),
             )
             a = dot(w2b[m, 0], dq[m, :, 0:1024], 1, 0)
             a = a + dot(w2b[m, 1], dq[m, :, 128:1152], 1, 0)
@@ -672,8 +682,8 @@
             pltpu.VMEM((4, 192, 1280), BF16),
             pltpu.VMEM((4, 64, 1024), F32),
             pltpu.VMEM((2, 4, 1, 256), F32),
-            pltpu.VMEM((3, 2, 64, 128), F32),
-            pltpu.VMEM((3, 2, 6, 64, 128), F32),
+            pltpu.VMEM((3, 2, 2, 16, 128), F32),
+            pltpu.VMEM((3, 2, 6, 16, 128), F32),
             pltpu.VMEM((8, 16, 8, 128), F32),
             pltpu.VMEM((8, 16, 8, 128), F32),
             pltpu.VMEM((64, 256), F32),
@@ -697,7 +707,7 @@
             pltpu.VMEM((2, 16, WHOLE, 128), F32),
             pltpu.VMEM((2, 16, 128), F32),
             pltpu.VMEM((4, 64, 1024), F32),
-            pltpu.VMEM((2, 4, 6, 64, 128), F32),
+            pltpu.VMEM((2, 4, 64, 128), F32),
             pltpu.VMEM((12, 4, 64, 1), F32),
             pltpu.SemaphoreType.DMA((20,)),
             pltpu.SemaphoreType.DMA((4,)),

time: 81.3 us -> 74.2 us (0.913)
  Pallas kernels: 80.4 us -> 73.3 us
    pallas_call x1, Pallas kernels: 78.2 us -> 71.2 us  [body(): pl.pallas_call(kernel, out_shape=(sds((4, 256, 8, 128), BF16), sds((2, 16...]
where the time goes in v6:
time: 74.2 us
  Pallas kernels  73.3 us (99%)
  between operations  0.82 us (1%)
    pallas_call x1, Pallas kernels, body(): pl.pallas_call(kernel, out_shape=(sds((4, 256, 8, 128), BF16), sds((2, 16...  71.2 us
    pallas_call x1, Pallas kernels, body(): pl.pallas_call(unpack, out_shape=(sds((4, 256, 8, 128), BF16), sds((64, 2...  2.13 us

profile of v6, /device:TPU:1, one launch (start us, length us, event | category | flops | bytes accessed | tf_op | source)
XLA Modules:
  0.0 74.2 jit_solution(8681662966368221348)
XLA Ops:
  0.6 71.2 %step.1 = (bf16[4,256,8,128]{3,2,1,0:T(8,128)(2,1)S(1)}, f32[2,16,24,128]{3,2,1,0:T(8,128)S(1)}, f32[2,16,8,128]{3,2,1,0:T(8,128)S(1)}, f32[8,128]{1,0:T(8,128)S(1)}) custom-call(bf16[4,256,8,128]{3,2,1,0:T(8,128)(2,1)} %x_hbm.1, bf16[4,256,8,128]{3,2,1,0:T(8,128)(2,1)} %c_hbm.1, bf16[64,256]{1,0:T(8,128)(2,1)} %bitcast.10, bf16[9,64,64]{2,1,0:T(8,128)(2,1)} %sw_hbm.1, ...), custom_call_target="tpu_custom_call" | custom-call | tf_op jit(solution)/shard_map/step/pallas_call | solution.py:647
  71.9 2.1 %unpack.1 = (bf16[4,256,8,128]{3,2,1,0:T(8,128)(2,1)}, f32[64,256]{1,0:T(8,128)}, f32[9,64,64]{2,1,0:T(8,128)}, f32[64,256]{1,0:T(8,128)}, f32[4,256]{1,0:T(4,12...) custom-call(bf16[4,256,8,128]{3,2,1,0:T(8,128)(2,1)S(1)} %get-tuple-, ...), custom_call_target="tpu_custom_call" | custom-call | tf_op jit(solution)/shard_map/unpack/pallas_call | solution.py:731

commit v7 on v6

--- a/solution.py
+++ b/solution.py
@@ -42,6 +42,22 @@
     for k in range(1, n):
         t = t + buf[k]
     return t
+
+
+class Rows:
+    def __init__(self, row, up, down):
+        self.row, self.up, self.down = row, up, down
+
+    def wait(self):
+        @pl.when(self.row > 0)
+        def _():
+            self.up.wait_send()
+            self.down.wait_recv()
+
+        @pl.when(self.row < 7)
+        def _():
+            self.down.wait_send()
+            self.up.wait_recv()
 
 
 def kernel(
@@ -178,7 +194,7 @@
             pltpu.make_async_remote_copy(
                 src_ref=hb.at[k, members, :, pl.ds(1024, 128)],
                 dst_ref=hb.at[k, members, :, pl.ds(0, 128)],
-                send_sem=hs_sem.at[t, 0], recv_sem=hr_sem.at[t, 0],
+                send_sem=hs_sem.at[t, 2], recv_sem=hr_sem.at[t, 2],
                 device_id=at(1, 0), device_id_type=MESH,
             ),
         ]
@@ -189,12 +205,12 @@
                     recv_sem=hr_sem.at[t, 1], device_id=at(*side), device_id_type=MESH,
                 )
             )
-        for copy in copies:
+        up, down = copies[:2]
+        pl.when(row > 0)(up.start)
+        pl.when(row < 7)(down.start)
+        for copy in copies[2:]:
             copy.start()
-        return [
-            together(hb.at[k, :, :, pl.ds(0, 128)], hs_sem.at[t, 0], hr_sem.at[t, 0]),
-            together(pr.at[k, n], hs_sem.at[t, 1], hr_sem.at[t, 1]),
-        ]
+        return [Rows(row, up, down), together(pr.at[k, n], hs_sem.at[t, 1], hr_sem.at[t, 1])]
 
     lane = lax.broadcasted_iota(jnp.int32, (64, 128), 1)
     sub = lax.broadcasted_iota(jnp.int32, (8, 128), 0)
@@ -238,6 +254,7 @@
     bottom = jnp.where(row < 7, 1.0, 0.0).astype(F32)
     left = jnp.where(col > 0, 1.0, 0.0).astype(F32)
     right = jnp.where(col < 31, 1.0, 0.0).astype(F32)
+    place_row = jnp.full((64, 128), row, jnp.int32)
     inside = zero
     for edge, value in enumerate((left, right, top * left, top * right, bottom * left, bottom * right)):
         inside = jnp.where((lane >= edge * 16) & (lane < edge * 16 + 16), value, inside)
@@ -247,9 +264,9 @@
         for i in range(10):
             t = tile(i)
             if i == 0:
-                t, first, at_row = t * top, 2, 7
+                t, first, at_row = jnp.where(place_row > 0, t, 0.0), 2, 7
             elif i == 9:
-                t, first, at_row = t * bottom, 4, 0
+                t, first, at_row = jnp.where(place_row < 7, t, 0.0), 4, 0
             else:
                 first, at_row = 0, i - 1
             where0 = first * 16 + m % 2 * 8 + at_row
@@ -713,8 +730,8 @@
             pltpu.SemaphoreType.DMA((4,)),
             pltpu.SemaphoreType.DMA((24,)),
             pltpu.SemaphoreType.DMA((24,)),
-            pltpu.SemaphoreType.DMA((6, 2)),
-            pltpu.SemaphoreType.DMA((6, 2)),
+            pltpu.SemaphoreType.DMA((6, 3)),
+            pltpu.SemaphoreType.DMA((6, 3)),
             pltpu.SemaphoreType.DMA((6,)),
             pltpu.SemaphoreType.DMA((6,)),
         ],

time: 74.2 us -> 74.5 us (level)
  no operation moved by 1% of the time
where the time goes in v7:
time: 74.5 us; the launch traced here: 74.4 us
  Pallas kernels  73.6 us (99%)
  between operations  0.82 us (1%)
    pallas_call x1, Pallas kernels, body(): pl.pallas_call(kernel, out_shape=(sds((4, 256, 8, 128), BF16), sds((2, 16...  71.5 us
    pallas_call x1, Pallas kernels, body(): pl.pallas_call(unpack, out_shape=(sds((4, 256, 8, 128), BF16), sds((64, 2...  2.13 us

profile of v7, /device:TPU:1, one launch (start us, length us, event | category | flops | bytes accessed | tf_op | source)
XLA Modules:
  0.0 74.4 jit_solution(12613818025824283321)
XLA Ops:
  0.6 71.5 %step.1 = (bf16[4,256,8,128]{3,2,1,0:T(8,128)(2,1)S(1)}, f32[2,16,24,128]{3,2,1,0:T(8,128)S(1)}, f32[2,16,8,128]{3,2,1,0:T(8,128)S(1)}, f32[8,128]{1,0:T(8,128)S(1)}) custom-call(bf16[4,256,8,128]{3,2,1,0:T(8,128)(2,1)} %x_hbm.1, bf16[4,256,8,128]{3,2,1,0:T(8,128)(2,1)} %c_hbm.1, bf16[64,256]{1,0:T(8,128)(2,1)} %bitcast.10, bf16[9,64,64]{2,1,0:T(8,128)(2,1)} %sw_hbm.1, ...), custom_call_target="tpu_custom_call" | custom-call | tf_op jit(solution)/shard_map/step/pallas_call | solution.py:664
  72.1 2.1 %unpack.1 = (bf16[4,256,8,128]{3,2,1,0:T(8,128)(2,1)}, f32[64,256]{1,0:T(8,128)}, f32[9,64,64]{2,1,0:T(8,128)}, f32[64,256]{1,0:T(8,128)}, f32[4,256]{1,0:T(4,12...) custom-call(bf16[4,256,8,128]{3,2,1,0:T(8,128)(2,1)S(1)} %get-tuple-, ...), custom_call_target="tpu_custom_call" | custom-call | tf_op jit(solution)/shard_map/unpack/pallas_call | solution.py:748
